TPU v7x, 32 devices: a whole 2x2x4 slice. The times are simulated.
32 devices in a mesh: sta: 8 (over z, y), yr: 4 (over x, core).
Axes of the slice: x: 2, y: 2, z: 4, core: 2. Of those that a mesh axis runs over, the one named last changes fastest.
Arguments:
- temps: float32 [196608, 128], P(('sta', 'yr')), may hold values from -6 to 6
- day_bits: int32 [4, 196608], P(None, ('sta', 'yr')), may hold values from -2147483648 to 2147483646, as said below
- block_offset: int32 [196608], P(('sta', 'yr')), may hold values from 0 to 47
- block_counts: int32 [4, 2048], P('yr', 'sta'), may hold values from 0 to 48, as said below
- station_cell: int32 [2048], P('sta'), may hold values from 0 to 10367, as said below
Outputs:
- anomalies: float32 [196608, 128], P(('sta', 'yr'))
- climatology: float32 [10368, 384], P('sta')
Inputs may be any that keep to these rules, and one draw needn't show every extreme that they name: `day_bits`: bit i of word w of a block's column says whether day 32 * w + i of the block was observed. `block_counts`: for each year range and station shard, the counts of the shard's 256 stations sum to 6144; in each of them some station has 48. `station_cell`: the owner of cell c is c // 1296. Of the 256 stations of one shard at most 128 lie in cells of one owner, and one owner has exactly 128 stations of every shard.
All inputs are finite; a program needn't handle non-finite values.
Results may differ from a plain program's by a relative error of at most 0.0003.
Values sent between devices are 32-bit elements; how exact they have to be, the bound alone decides.
A program may use at most 128 MiB of HBM per device.

v0:
```python
import functools

import jax
import jax.numpy as jnp
from jax import lax
from jax.experimental import pallas as pl
from jax.experimental.pallas import tpu as pltpu
from jax.sharding import PartitionSpec as P

CELLS = 10368
CALENDAR = 365
MOST_BLOCKS = 48
LANES = 128
F32 = jnp.float32
BF16 = jnp.bfloat16


def round_up(value, step):
    return (value + step - 1) // step * step


def day_code(bits, offsets):
    rows = bits.shape[1]
    third = offsets - 3 * ((offsets * 21846) >> 16)
    words = jnp.concatenate(
        [jnp.broadcast_to(bits[w : w + 1], (32, rows)) for w in range(bits.shape[0])], axis=0
    )
    day = lax.broadcasted_iota(jnp.int32, words.shape, 0)
    bit = (words >> (day & 31)) & 1
    observed = jnp.where(third * LANES + day < CALENDAR, bit, 0)
    return third, (observed + 2 * third).astype(F32)


def split_two(value):
    high = value.astype(BF16)
    return high, (value - high.astype(F32)).astype(BF16)


def lane_group(rows, width):
    return lax.broadcasted_iota(jnp.int32, (rows, LANES), 1) // width


def gather_lanes(parts, shifts, width):
    group = lane_group(parts[0].shape[0], width)
    total = None
    for j, (part, shift) in enumerate(zip(parts, shifts)):
        shift = shift % LANES
        moved = pltpu.roll(part, shift, 1) if shift else part
        total = jnp.where(group == j, moved, 0.0 if total is None else total)
    return total


def sums_kernel(ranges, packed, temps_ref, bits_ref, offs_ref, counts_ref, out_ref, acc, edges):
    step = pl.program_id(0)
    rows = temps_ref.shape[0]
    stations = counts_ref.shape[1]

    @pl.when(step == 0)
    def _():
        acc[...] = jnp.zeros_like(acc)
        counts = jnp.broadcast_to(counts_ref[...].astype(F32), (stations, stations))
        at = lax.broadcasted_iota(jnp.int32, (stations, stations), 0)
        of = lax.broadcasted_iota(jnp.int32, (stations, stations), 1)
        ends = jnp.sum(jnp.where(of <= at, counts, 0.0), axis=1, keepdims=True)
        starts = jnp.sum(jnp.where(of < at, counts, 0.0), axis=1, keepdims=True)
        edges[0] = jnp.broadcast_to(starts, (stations, LANES)).astype(jnp.int32)
        edges[1] = jnp.broadcast_to(ends, (stations, LANES)).astype(jnp.int32)

    third, code = day_code(bits_ref[...], offs_ref[...])
    code = code.T
    observed = code - 2.0 * jnp.floor(code * 0.5)
    high, low = split_two(temps_ref[...] * observed)
    values = jnp.concatenate([high, low, observed.astype(BF16)], axis=1)
    row = lax.broadcasted_iota(jnp.int32, (1, rows), 1) + step * rows
    inside = (row >= edges[0][:, 0:1]) & (row < edges[1][:, 0:1])
    station_third = jnp.where(inside, third, 3)
    onehot = jnp.concatenate(
        [jnp.where(station_third == k, 1.0, 0.0).astype(BF16) for k in range(3)], axis=0
    )
    acc[...] += jnp.dot(onehot, values, preferred_element_type=F32)

    @pl.when(step == pl.num_programs(0) - 1)
    def _():
        width = LANES // ranges
        third_of = [acc[k * stations : (k + 1) * stations, :] for k in range(3)]
        groups = [t[:, :LANES] + t[:, LANES : 2 * LANES] for t in third_of]
        tallies = [t[:, 2 * LANES :] for t in third_of]
        if packed:
            groups.append(tallies[0] + 256.0 * tallies[1] + 65536.0 * tallies[2])
        else:
            groups.extend(tallies)
        for r in range(ranges):
            out_ref[r] = gather_lanes(groups, [width * (k - r) for k in range(len(groups))], width)


def cell_chunks(ranges, cell_pad, stations):
    cell_rows, station_rows = cell_pad // ranges, stations // ranges
    step = round_up((cell_rows + 2) // 3, 8)
    edges = [*range(0, cell_rows, step), cell_rows]
    return [(cell_rows, cell_rows + station_rows)] + list(zip(edges[:-1], edges[1:]))


def cells_kernel(
    ranges, packed, cell_dev, cell_pad, got_ref, own_ref, out_ref, values, acc,
    far_send, far_recv, near_send, near_recv,
):
    shards, _, _ = got_ref.shape
    stations = own_ref.shape[0]
    width = LANES // ranges
    chips = ranges // 2
    yr = lax.axis_index("yr")
    chip, core = yr // 2, lax.rem(yr, 2)
    partner = {"yr": chip * 2 + 1 - core}
    others = [lax.rem(chip + k, chips) * 2 + core for k in range(1, chips)]
    origins = [lax.rem(chip + chips - k, chips) * 2 + core for k in range(1, chips)]
    greet([partner] + [{"yr": other} for other in others])
    group = lane_group(stations, width)
    for s in range(shards):
        both = got_ref[s, :stations, :]
        high, low = split_two(both)
        if packed:
            tally = both.astype(jnp.int32)
            tally = jnp.where(
                group == 0,
                pltpu.roll(tally, LANES - 3 * width, 1) & 255,
                jnp.where(
                    group == 1,
                    (pltpu.roll(tally, LANES - 2 * width, 1) >> 8) & 255,
                    (pltpu.roll(tally, LANES - width, 1) >> 16) & 255,
                ),
            ).astype(F32)
            columns = [high, low, tally.astype(BF16)]
        else:
            tally = pltpu.roll(both, LANES - 3 * width, 1)
            columns = [high, low, *split_two(tally)]
        values[s * stations : (s + 1) * stations] = jnp.concatenate(columns, axis=1)
    first = lax.axis_index("sta") * cell_dev
    cell_rows = cell_pad // ranges
    fars, nears = [], []
    for c, (low_row, high_row) in enumerate(cell_chunks(ranges, cell_pad, stations)):
        count = high_row - low_row
        if low_row == cell_rows:
            ids = own_ref[...]
        else:
            ids = jnp.concatenate(
                [
                    lax.broadcasted_iota(jnp.int32, (count, 1), 0) + (first + j * cell_rows + low_row)
                    for j in range(ranges)
                ],
                axis=0,
            ).astype(F32)
        total = ranges * count
        acc[:total] = jnp.zeros((total, acc.shape[1]), F32)
        for s in range(shards):
            hot = jnp.concatenate(
                [
                    jnp.where(ids == got_ref[s, q : q + 1, :], 1.0, 0.0).astype(BF16)
                    for q in range(stations, stations + stations // LANES)
                ],
                axis=1,
            )
            acc[:total] += jnp.dot(
                hot, values[s * stations : (s + 1) * stations], preferred_element_type=F32
            )
        tallies = acc[:total, 2 * LANES : 3 * LANES]
        if not packed:
            tallies = tallies + acc[:total, 3 * LANES :]
        clim = (acc[:total, :LANES] + acc[:total, LANES : 2 * LANES]) / jnp.maximum(tallies, 1.0)
        for k in range(3):
            out_ref[yr, k, low_row:high_row] = gather_lanes(
                [clim[j * count : (j + 1) * count] for j in range(ranges)],
                [width * (j - k) for j in range(ranges)],
                width,
            )
        block = out_ref.at[yr, :, low_row:high_row, :]
        for k, other in enumerate(others):
            copy = remote(block, block, far_send.at[c, k], far_recv.at[c, k], {"yr": other})
            copy.start()
            fars.append(copy)
        copy = remote(block, block, near_send.at[c, chips - 1], near_recv.at[c, chips - 1], partner)
        copy.start()
        nears.append(copy)
    for c, (low_row, high_row) in enumerate(cell_chunks(ranges, cell_pad, stations)):
        for k, origin in enumerate(origins):
            fars[c * len(origins) + k].wait_recv()
            block = out_ref.at[origin, :, low_row:high_row, :]
            copy = remote(block, block, near_send.at[c, k], near_recv.at[c, k], partner)
            copy.start()
            nears.append(copy)
    for copy in nears:
        copy.wait_recv()
    for copy in fars + nears:
        copy.wait_send()


def unpack(clim_ref, k, j, first, count, ranges, width):
    return gather_lanes(
        [clim_ref[r, k, first : first + count, :] for r in range(ranges)],
        [width * (r - j) for r in range(ranges)],
        width,
    )


def anomaly_kernel(
    ranges, cell_dev, cell_pad, temps_ref, bits_ref, offs_ref, counts_ref, clim_ref,
    out_ref, climatology_ref, edges, table,
):
    step = pl.program_id(0)
    rows = temps_ref.shape[0]
    stations = counts_ref.shape[1]
    width = LANES // ranges
    cell_rows, station_rows = cell_pad // ranges, stations // ranges

    @pl.when(step == 0)
    def _():
        at = lax.broadcasted_iota(jnp.int32, (stations, stations), 0)
        of = lax.broadcasted_iota(jnp.int32, (stations, stations), 1)
        counts = jnp.broadcast_to(counts_ref[...].astype(F32), (stations, stations))
        column = jnp.sum(jnp.where(at == of, counts, 0.0), axis=1, keepdims=True)
        ends = jnp.sum(jnp.where(at <= of, column, 0.0), axis=0, keepdims=True)
        edges[0:1] = (ends - counts_ref[...].astype(F32)).astype(jnp.int32)
        edges[1:2] = ends.astype(jnp.int32)
        for k in range(3):
            for j in range(ranges):
                part = unpack(clim_ref, k, j, cell_rows, station_rows, ranges, width)
                high, low = split_two(part)
                at_rows = slice(j * station_rows, (j + 1) * station_rows)
                table[at_rows, 2 * k * LANES : (2 * k + 1) * LANES] = high
                table[at_rows, (2 * k + 1) * LANES : (2 * k + 2) * LANES] = low
                count = min(cell_dev - j * cell_rows, cell_rows)
                if count > 0:
                    climatology_ref[
                        j * cell_rows : j * cell_rows + count, k * LANES : (k + 1) * LANES
                    ] = unpack(clim_ref, k, j, 0, count, ranges, width)

    _, code = day_code(bits_ref[...], offs_ref[...])
    code = code.T
    third = jnp.floor(code * 0.5)
    row = lax.broadcasted_iota(jnp.int32, (rows, stations), 0) + step * rows
    inside = (row >= edges[0:1]) & (row < edges[1:2])
    onehot = jnp.where(inside, 1.0, 0.0).astype(BF16)
    found = jnp.dot(onehot, table[...], preferred_element_type=F32)
    clim = [
        found[:, 2 * k * LANES : (2 * k + 1) * LANES]
        + found[:, (2 * k + 1) * LANES : (2 * k + 2) * LANES]
        for k in range(3)
    ]
    block_clim = jnp.where(third == 0.0, clim[0], jnp.where(third == 1.0, clim[1], clim[2]))
    out_ref[...] = (code - 2.0 * third) * (temps_ref[...] - block_clim)


def remote(src, dst, send, recv, where):
    return pltpu.make_async_remote_copy(
        src_ref=src, dst_ref=dst, send_sem=send, recv_sem=recv,
        device_id=where, device_id_type=pl.DeviceIdType.MESH,
    )


def greet(peers, maybe=(), maybe_count=0):
    barrier = pltpu.get_barrier_semaphore()
    for where in peers:
        pl.semaphore_signal(barrier, inc=1, device_id=where, device_id_type=pl.DeviceIdType.MESH)
    for able, where in maybe:
        @pl.when(able)
        def _():
            pl.semaphore_signal(
                barrier, inc=1, device_id=where, device_id_type=pl.DeviceIdType.MESH
            )
    pl.semaphore_wait(barrier, len(peers) + maybe_count)


def gather_kernel(
    owners, ranges, major, sums_ref, cells_ref, out_ref, pair, partial, across,
    pair_send, pair_recv, across_send, across_recv, far_send, far_recv, near_send, near_recv,
):
    stations = sums_ref.shape[1]
    chips, minor = ranges // 2, owners // major
    sta, yr = lax.axis_index("sta"), lax.axis_index("yr")
    chip, core = yr // 2, lax.rem(yr, 2)
    row, place = sta // minor, lax.rem(sta, minor)
    partner = {"yr": chip * 2 + 1 - core}
    chip_at = [lax.rem(chip + k, chips) for k in range(chips)]
    chip_from = [lax.rem(chip + chips - k, chips) for k in range(chips)]
    near_peers = [{"sta": row * minor + lax.rem(place + j, minor)} for j in range(1, minor)]
    can_up, can_down = row < major - 1, row > 0

    def up(d):
        block = out_ref.at[(row - (d - 1)) * minor + place]
        return remote(
            block, block, far_send.at[0, d - 1], far_recv.at[0, d - 1],
            {"sta": (row + 1) * minor + place},
        )

    def down(d):
        block = out_ref.at[(row + (d - 1)) * minor + place]
        return remote(
            block, block, far_send.at[1, d - 1], far_recv.at[1, d - 1],
            {"sta": (row - 1) * minor + place},
        )

    def near(side, d):
        block = out_ref.at[(row + (d if side else -d)) * minor + place]
        return [
            remote(
                block, block, near_send.at[side, d, j], near_recv.at[side, d, j], near_peers[j]
            )
            for j in range(minor - 1)
        ]

    greet(
        [partner] + [{"yr": c * 2 + core} for c in chip_at[1:]] + near_peers,
        [
            (can_up, {"sta": (row + 1) * minor + place}),
            (can_down, {"sta": (row - 1) * minor + place}),
        ],
        (2 * (major - 1) - row) // major + (row + major - 1) // major,
    )

    pairs = []
    for k in [*range(1, chips), 0]:
        copy = remote(
            sums_ref.at[chip_at[k] * 2 + 1 - core], pair.at[k],
            pair_send.at[k], pair_recv.at[k], partner,
        )
        copy.start()
        pairs.append(copy)
    crossing = []
    for k in range(1, chips):
        pairs[k - 1].wait_recv()
        partial[k - 1] = sums_ref[chip_at[k] * 2 + core] + pair[k]
        copy = remote(
            partial.at[k - 1], across.at[k - 1], across_send.at[k - 1], across_recv.at[k - 1],
            {"yr": chip_at[k] * 2 + core},
        )
        copy.start()
        crossing.append(copy)
    pairs[-1].wait_recv()
    total = sums_ref[yr] + pair[0]
    for k, copy in enumerate(crossing):
        copy.wait_recv()
        total = total + across[k]
    out_ref[sta, :stations] = total
    out_ref[sta, stations:] = cells_ref[...]

    for able, copy_of in ((can_up, up), (can_down, down)):
        @pl.when(able)
        def _():
            copy_of(1).start()
    for copy in near(0, 0):
        copy.start()
    for d in range(1, major):
        for side, have, able, copy_of in (
            (0, row >= d, can_up, up), (1, row + d < major, can_down, down)
        ):
            @pl.when(have)
            def _():
                copy_of(d).wait_recv()
                if d + 1 < major:
                    @pl.when(able)
                    def _():
                        copy_of(d + 1).start()
                for copy in near(side, d):
                    copy.start()
    for copy in near(0, 0):
        copy.wait()
    for d in range(1, major):
        for side, have, able, copy_of in (
            (0, row >= d, can_up, up), (1, row + d < major, can_down, down)
        ):
            @pl.when(have)
            def _():
                for copy in near(side, d):
                    copy.wait()
            reach = (row >= d - 1) if side == 0 else (row + d - 1 < major)

            @pl.when(reach & able)
            def _():
                copy_of(d).wait_send()
    for copy in pairs + crossing:
        copy.wait_send()


def exchange_in(sums, cells, owners, ranges):
    stations = sums.shape[1]
    major = 4 if owners % 4 == 0 else owners
    chips, minor = ranges // 2, owners // major
    block = stations + cells.shape[0]
    dma = pltpu.SemaphoreType.DMA
    hops, near_count = max(major - 1, 1), max(minor - 1, 1)
    crossings = max(chips - 1, 1)
    return pl.pallas_call(
        functools.partial(gather_kernel, owners, ranges, major),
        in_specs=[pl.BlockSpec(memory_space=pltpu.VMEM)] * 2,
        out_specs=pl.BlockSpec(memory_space=pltpu.VMEM),
        out_shape=jax.ShapeDtypeStruct((owners, block, LANES), F32),
        scratch_shapes=[
            pltpu.VMEM((chips, stations, LANES), F32),
            pltpu.VMEM((crossings, stations, LANES), F32),
            pltpu.VMEM((crossings, stations, LANES), F32),
            dma((chips,)), dma((chips,)), dma((crossings,)), dma((crossings,)),
            dma((2, hops)), dma((2, hops)), dma((2, major, near_count)), dma((2, major, near_count)),
        ],
        compiler_params=pltpu.CompilerParams(
            collective_id=0, has_side_effects=True, vmem_limit_bytes=48 * 1024 * 1024
        ),
    )(sums, cells)


def per_device(temps, day_bits, block_offset, block_counts, station_cell):
    owners, ranges = lax.axis_size("sta"), lax.axis_size("yr")
    stations = station_cell.shape[0]
    block_total, day_count = temps.shape
    cell_dev = CELLS // owners
    cell_pad = round_up(cell_dev, 8 * ranges)
    packed = ranges * MOST_BLOCKS < 256
    rows = 1024 if block_total % 1024 == 0 else block_total
    offsets = block_offset.reshape(1, block_total)
    row_specs = [
        pl.BlockSpec((rows, day_count), lambda i: (i, 0)),
        pl.BlockSpec((day_bits.shape[0], rows), lambda i: (0, i)),
        pl.BlockSpec((1, rows), lambda i: (0, i)),
        pl.BlockSpec((1, stations), lambda i: (0, 0)),
    ]
    params = pltpu.CompilerParams(
        dimension_semantics=("arbitrary",), vmem_limit_bytes=48 * 1024 * 1024
    )
    sums = pl.pallas_call(
        functools.partial(sums_kernel, ranges, packed),
        grid=(block_total // rows,),
        in_specs=row_specs,
        out_specs=pl.BlockSpec((ranges, stations, LANES), lambda i: (0, 0, 0)),
        out_shape=jax.ShapeDtypeStruct((ranges, stations, LANES), F32),
        scratch_shapes=[
            pltpu.VMEM((3 * stations, 3 * LANES), F32),
            pltpu.VMEM((2, stations, LANES), jnp.int32),
        ],
        compiler_params=params,
    )(temps, day_bits, offsets, block_counts)

    cell_row_count = round_up(stations // LANES, 8)
    cell_rows = jnp.pad(
        station_cell.astype(F32).reshape(stations // LANES, LANES),
        ((0, cell_row_count - stations // LANES), (0, 0)),
    )
    got = exchange_in(sums, cell_rows, owners, ranges)

    part_rows = (cell_pad + stations) // ranges
    chunks = cell_chunks(ranges, cell_pad, stations)
    most = max(high - low for low, high in chunks)
    columns = (3 if packed else 4) * LANES
    dma = pltpu.SemaphoreType.DMA
    hops = (len(chunks), max(ranges // 2 - 1, 1))
    steps = (len(chunks), ranges // 2)
    parts = pl.pallas_call(
        functools.partial(cells_kernel, ranges, packed, cell_dev, cell_pad),
        in_specs=[pl.BlockSpec(memory_space=pltpu.VMEM)] * 2,
        out_specs=pl.BlockSpec(memory_space=pltpu.VMEM),
        out_shape=jax.ShapeDtypeStruct((ranges, 3, part_rows, LANES), F32),
        scratch_shapes=[
            pltpu.VMEM((owners * stations, columns), BF16),
            pltpu.VMEM((ranges * most, columns), F32),
            dma(hops), dma(hops), dma(steps), dma(steps),
        ],
        compiler_params=pltpu.CompilerParams(
            collective_id=1, has_side_effects=True, vmem_limit_bytes=48 * 1024 * 1024
        ),
    )(got, station_cell.astype(F32).reshape(stations, 1))

    return pl.pallas_call(
        functools.partial(anomaly_kernel, ranges, cell_dev, cell_pad),
        grid=(block_total // rows,),
        in_specs=row_specs
        + [pl.BlockSpec((ranges, 3, part_rows, LANES), lambda i: (0, 0, 0, 0))],
        out_specs=[
            pl.BlockSpec((rows, day_count), lambda i: (i, 0)),
            pl.BlockSpec((cell_dev, 3 * LANES), lambda i: (0, 0)),
        ],
        out_shape=[
            jax.ShapeDtypeStruct((block_total, day_count), F32),
            jax.ShapeDtypeStruct((cell_dev, 3 * LANES), F32),
        ],
        scratch_shapes=[
            pltpu.VMEM((8, stations), jnp.int32),
            pltpu.VMEM((stations, 6 * LANES), BF16),
        ],
        compiler_params=params,
    )(temps, day_bits, offsets, block_counts, parts)


def solution(mesh):
    in_specs = (
        P(("sta", "yr"), None),
        P(None, ("sta", "yr")),
        P(("sta", "yr")),
        P("yr", "sta"),
        P("sta"),
    )
    out_specs = (P(("sta", "yr"), None), P("sta", None))

    def run(*args):
        return tuple(per_device(*args))

    return jax.shard_map(
        run, mesh=mesh, in_specs=in_specs, out_specs=out_specs, check_vma=False
    )
```

profile of v0, /device:TPU:0, one launch (start us, length us, event | category | flops | bytes accessed | tf_op | source)
XLA Modules:
  0.0 67.0 jit_solution(12944532487153054005)
XLA Ops:
  0.6 0.7 %fusion = (f32[256]{0:T(256)S(1)}, f32[2,128]{1,0:T(2,128)S(1)}) fusion(s32[256]{0:T(256)} %param.9), kind=kLoop, calls=%fused_computation.1 | loop fusion | flops 256 | bytes 3072 | tf_op jit(solution)/shard_map/convert_element_type | solution.py:442
  1.3 0.1 copy.7.own_ref
  1.5 0.0 copy-start
  1.5 1.9 %copy-done = f32[6144,128]{1,0:T(8,128)S(1)} copy-done((f32[6144,128]{1,0:T(8,128)S(1)}, f32[6144,128]{1,0:T(8,128)}, u32[]{:S(2)}) %copy-start) | copy-done | bytes 3145752
  3.4 0.0 copy-start.2
  3.4 0.9 %copy-done.2 = s32[4,6144]{1,0:T(4,128)S(1)} copy-done((s32[4,6144]{1,0:T(4,128)S(1)}, s32[4,6144]{1,0:T(4,128)}, u32[]{:S(2)}) %copy-start.2) | copy-done | bytes 98328
  4.2 0.0 copy-start.3
  4.3 0.7 %copy-done.3 = s32[6144]{0:T(1024)S(1)} copy-done((s32[6144]{0:T(1024)S(1)}, s32[6144]{0:T(1024)}, u32[]{:S(2)}) %copy-start.3) | copy-done | bytes 24600
  5.0 0.0 copy-start.4
  5.0 0.7 %copy-done.4 = s32[1,256]{1,0:T(1,128)S(1)} copy-done((s32[1,256]{1,0:T(1,128)S(1)}, s32[1,256]{1,0:T(1,128)}, u32[]{:S(2)}) %copy-start.4) | copy-done | bytes 1048
  5.7 7.3 %shard_map.68.sums_ref = f32[4,256,128]{2,1,0:T(8,128)S(1)} custom-call(f32[6144,128]{1,0:T(8,128)S(1)} %copy-done, s32[4,6144]{1,0:T(4,128)S(1)} %copy-done.2, s32[1,6144]{1,0:T(1,128)S(1)} %bitcast.4, s32[1,256]{1,0:T(1,128)S(1)} %copy-done.4), custom_call_target="tpu_custom_call" | custom-call | tf_op jit(solution)/shard_map/pallas_call | solution.py:427
  13.0 0.0 copy-start.1
  13.0 27.9 %shard_map.69.got_ref = f32[8,264,128]{2,1,0:T(8,128)S(1)} custom-call(f32[4,256,128]{2,1,0:T(8,128)S(1)} %shard_map.68.sums_ref, f32[8,128]{1,0:T(8,128)S(1)} %pad.4.cells_ref), custom_call_target="tpu_custom_call" | custom-call | tf_op jit(solution)/shard_map/pallas_call | solution.py:391
  40.9 18.2 %shard_map.70.clim_ref = f32[4,3,392,128]{3,2,1,0:T(8,128)S(1)} custom-call(f32[8,264,128]{2,1,0:T(8,128)S(1)} %shard_map.69.got_ref, f32[256,1]{1,0:T(8,128)S(1)} %copy.7.own_ref), custom_call_target="tpu_custom_call" | custom-call | tf_op jit(solution)/shard_map/pallas_call | solution.py:454
  59.1 0.0 copy-done.1
  59.2 7.8 %shard_map.71 = (f32[6144,128]{1,0:T(8,128)}, f32[1296,384]{1,0:T(8,128)}) custom-call(f32[6144,128]{1,0:T(8,128)S(1)} %copy-done.1, s32[4,6144]{1,0:T(4,128)S(1)} %copy-done.2, s32[1,6144]{1,0:T(1,128)S(1)} %bitcast.5, s32[1,256]{1,0:T(1,128)S(1)} %copy-done.4, f32[4,3,392,128]{3,2,1,0:T(8,128)S(1)} %shard_map.70.clim_ref), custom_call_target="tpu_custom_call" | custom-call | tf_op jit(solution)/shard_map/pallas_call | solution.py:469
  (1 shorter events, 0.0 us)
Async XLA Ops:
  1.5 1.9 %copy-start = (f32[6144,128]{1,0:T(8,128)S(1)}, f32[6144,128]{1,0:T(8,128)}, u32[]{:S(2)}) copy-start(f32[6144,128]{1,0:T(8,128)} %temps_ref.3) | copy-start | bytes 9437188
  3.4 0.9 %copy-start.2 = (s32[4,6144]{1,0:T(4,128)S(1)}, s32[4,6144]{1,0:T(4,128)}, u32[]{:S(2)}) copy-start(s32[4,6144]{1,0:T(4,128)} %bits_ref.3) | copy-start | bytes 294916
  4.2 0.7 %copy-start.3 = (s32[6144]{0:T(1024)S(1)}, s32[6144]{0:T(1024)}, u32[]{:S(2)}) copy-start(s32[6144]{0:T(1024)} %param.7) | copy-start | bytes 73732
  5.0 0.7 %copy-start.4 = (s32[1,256]{1,0:T(1,128)S(1)}, s32[1,256]{1,0:T(1,128)}, u32[]{:S(2)}) copy-start(s32[1,256]{1,0:T(1,128)} %counts_ref.3) | copy-start | bytes 3076
  13.0 46.2 %copy-start.1 = (f32[6144,128]{1,0:T(8,128)S(1)}, f32[6144,128]{1,0:T(8,128)}, u32[]{:S(2)}) copy-start(f32[6144,128]{1,0:T(8,128)} %temps_ref.3) | copy-start | bytes 9437188
where the time goes:
time: 67.3 us; the launch traced here: 67 us
  Pallas kernels  61.3 us (91%)
  local copies, waits for them, and re-layouts  4.34 us (6%)
  between operations  0.69 us (1%)
  other arithmetic  0.68 us (1%)
    pallas_call x1, Pallas kernels, exchange_in(): pl.pallas_call(functools.partial(gather_kernel, owners, ranges, major), i...  27.9 us
    pallas_call x1, Pallas kernels, per_device(): pl.pallas_call(functools.partial(cells_kernel, ranges, packed, cell_dev,...  18.2 us
    pallas_call x1, Pallas kernels, per_device(): pl.pallas_call(functools.partial(anomaly_kernel, ranges, cell_dev, cell_p...  7.84 us
    pallas_call x1, Pallas kernels, per_device(): pl.pallas_call(functools.partial(sums_kernel, ranges, packed), grid=(bloc...  7.31 us
    unnamed x10, local copies, waits for them, and re-layouts  4.2 us

commit v1 on v0

v1 whole, which is shorter than its diff:
```python
import functools

import jax
import jax.numpy as jnp
from jax import lax
from jax.experimental import pallas as pl
from jax.experimental.pallas import tpu as pltpu
from jax.sharding import PartitionSpec as P

CELLS = 10368
CALENDAR = 365
MOST_BLOCKS = 48
LANES = 128
TILE = 8
F32 = jnp.float32
BF16 = jnp.bfloat16
I32 = jnp.int32
VMEM = pltpu.VMEM


def round_up(value, step):
    return (value + step - 1) // step * step


def tally_words(ranges):
    if ranges * MOST_BLOCKS < 256:
        return [(0, 1, 2)], 256
    return [(0, 1), (2,)], 4096


def iota(shape, dim):
    return lax.broadcasted_iota(I32, shape, dim)


def one_where(mask):
    return jnp.where(mask, 1.0, 0.0).astype(BF16)


def dot(a, b, dims=((1,), (0,))):
    return lax.dot_general(a, b, (dims, ((), ())), preferred_element_type=F32)


def split_two(value):
    high = value.astype(BF16)
    return high, (value - high.astype(F32)).astype(BF16)


def row_stations(counts, blocks):
    stations = counts.shape[1]
    spread = jnp.broadcast_to(counts.astype(F32), (LANES, stations)).astype(BF16)
    square = (stations, stations)
    ends = dot(one_where(iota(square, 1) <= iota(square, 0)), spread, ((1,), (1,))).astype(I32)
    lane = iota((stations, LANES), 1)
    ending = dot(one_where((ends >> 7) == lane), one_where((ends & 127) == lane), ((0,), (0,)))
    ending = ending.astype(BF16)
    tile = (LANES, LANES)
    within = dot(ending, one_where(iota(tile, 0) <= iota(tile, 1)))
    totals = dot(ending, jnp.ones(tile, BF16)).astype(BF16)
    before = dot(one_where(iota(tile, 1) < iota(tile, 0)), totals)
    return (within + before)[:blocks]


def sums_kernel(
    ranges, rows, temps_hbm, bits_hbm, offs_hbm, counts_hbm, cell_hbm,
    sums_ref, masked_ref, code_ref, cells_ref, bits, offs, counts, acc, tally, small, large,
):
    block_total = masked_ref.shape[0]
    blocks, stations = offs.shape[0], counts.shape[1]
    words, base = tally_words(ranges)
    chunk_count = sums_ref.shape[1]
    firsts = [
        pltpu.make_async_copy(counts_hbm, counts, small.at[0]),
        pltpu.make_async_copy(offs_hbm, offs, small.at[1]),
        pltpu.make_async_copy(bits_hbm, bits, small.at[2]),
        pltpu.make_async_copy(cell_hbm, cells_ref.at[0 : cell_hbm.shape[0]], small.at[3]),
    ]
    steps = block_total // rows
    loads = [
        pltpu.make_async_copy(
            temps_hbm.at[i * rows : (i + 1) * rows], masked_ref.at[i * rows : (i + 1) * rows],
            large.at[i],
        )
        for i in range(steps)
    ]
    for copy in firsts + loads:
        copy.start()
    firsts[0].wait()
    station = row_stations(counts[...], blocks)
    firsts[1].wait()
    offsets = offs[...]
    third = offsets - 3 * ((offsets * 21846) >> 16)
    double_segment = 2 * (third * stations + station.astype(I32))
    limit = CALENDAR - LANES * third
    station_of = [jnp.where(third == k, station, -1.0).astype(BF16) for k in range(3)]
    weight_of = []
    for held in words:
        weight = jnp.zeros(third.shape, F32)
        for place, k in enumerate(held):
            weight = jnp.where(third == k, float(base**place), weight)
        weight_of.append(weight.astype(BF16))
    station = station.astype(BF16)
    at = iota((stations, LANES), 0).astype(F32).astype(BF16)
    day = iota((LANES, LANES), 0)
    shift = day & 31
    one, zero = jnp.ones((), BF16), jnp.zeros((), BF16)
    firsts[2].wait()
    for i in range(steps):
        loads[i].wait()
        values, observed_all, hots, weights = [], [], [], []
        for q in range(i * rows // LANES, (i + 1) * rows // LANES):
            here = slice(q * LANES, (q + 1) * LANES)
            packed = jnp.concatenate(
                [jnp.broadcast_to(bits[w : w + 1, here], (32, LANES)) for w in range(bits.shape[0])],
                axis=0,
            )
            bit = (packed >> shift) & 1
            code = jnp.where(day < limit[q : q + 1], bit, 0) + double_segment[q : q + 1]
            code = code.T
            code_ref[here] = code
            observed = (code & 1).astype(F32)
            value = masked_ref[here] * observed
            masked_ref[here] = value
            values.append(jnp.concatenate(split_two(value), axis=1))
            observed_all.append(observed.astype(BF16))
            hots.append(
                jnp.concatenate(
                    [
                        jnp.where(at == jnp.broadcast_to(s[q : q + 1], at.shape), one, zero)
                        for s in station_of
                    ],
                    axis=0,
                )
            )
            inside = at == jnp.broadcast_to(station[q : q + 1], at.shape)
            weights.append(
                jnp.concatenate(
                    [
                        jnp.where(inside, jnp.broadcast_to(w[q : q + 1], at.shape), zero)
                        for w in weight_of
                    ],
                    axis=0,
                )
            )
        total = dot(jnp.concatenate(hots, axis=1), jnp.concatenate(values, axis=0))
        count = dot(jnp.concatenate(weights, axis=1), jnp.concatenate(observed_all, axis=0))
        acc[...] = total if i == 0 else acc[...] + total
        tally[...] = count if i == 0 else tally[...] + count
    split = (ranges, chunk_count, TILE, stations)
    for k in range(3):
        part = acc[k * stations : (k + 1) * stations]
        sums_ref[:, :, k] = (part[:, :LANES] + part[:, LANES:]).T.reshape(split)
    for w in range(len(words)):
        sums_ref[:, :, 3 + w] = tally[w * stations : (w + 1) * stations].T.reshape(split)
    firsts[3].wait()


def remote(src, dst, send, recv, where):
    return pltpu.make_async_remote_copy(
        src_ref=src, dst_ref=dst, send_sem=send, recv_sem=recv,
        device_id=where, device_id_type=pl.DeviceIdType.MESH,
    )


def greet(peers):
    barrier = pltpu.get_barrier_semaphore()
    for where in peers:
        pl.semaphore_signal(barrier, inc=1, device_id=where, device_id_type=pl.DeviceIdType.MESH)
    pl.semaphore_wait(barrier, len(peers))


def pick(index, table):
    value = jnp.int32(table[0])
    for i in range(1, len(table)):
        value = jnp.where(index == i, jnp.int32(table[i]), value)
    return value


def exchange_kernel(
    ranges, owners, major, cell_dev, cell_pad, sums_ref, cells_ref, out_ref,
    ids, pair, partial, across, got, lhs, hot,
    id_send, id_recv, pair_send, pair_recv, across_send, across_recv,
    col_send, col_recv, row_send, row_recv, far_send, far_recv, near_send, near_recv,
):
    _, chunks, groups, _, stations = sums_ref.shape
    halves = stations // LANES
    words, base = tally_words(ranges)
    width = out_ref.shape[-1]
    chips, minor = ranges // 2, owners // major
    sta, yr = lax.axis_index("sta"), lax.axis_index("yr")
    chip, core = yr // 2, lax.rem(yr, 2)
    row, place = sta // minor, lax.rem(sta, minor)
    partner = {"yr": chip * 2 + 1 - core}
    chip_at = [lax.rem(chip + k, chips) for k in range(chips)]
    chip_from = [lax.rem(chip + chips - k, chips) for k in range(chips)]
    near_first = [
        sorted((r for r in range(major) if r != mine), key=lambda r: (abs(r - mine), r))
        for mine in range(major)
    ]
    rows_by = [pick(row, [near_first[m][i] for m in range(major)]) for i in range(major - 1)]

    greet(
        [partner]
        + [{"yr": c * 2 + core} for c in chip_at[1:]]
        + [{"sta": lax.rem(sta + j, owners)} for j in range(1, owners)]
    )
    id_copies = []
    for j in range(1, owners):
        copy = remote(
            cells_ref, ids.at[sta], id_send.at[j - 1], id_recv.at[j - 1],
            {"sta": lax.rem(sta + j, owners)},
        )
        copy.start()
        id_copies.append(copy)
    pairs = []
    for c in range(chunks):
        for k in [*range(1, chips), 0]:
            copy = remote(
                sums_ref.at[chip_at[k] * 2 + 1 - core, c], pair.at[c, k],
                pair_send.at[c, k], pair_recv.at[c, k], partner,
            )
            copy.start()
            pairs.append(copy)
    ids[sta] = cells_ref[...]
    crossing = []
    for c in range(chunks):
        for k in range(1, chips):
            pairs[c * chips + k - 1].wait_recv()
            partial[c, k - 1] = sums_ref[chip_at[k] * 2 + core, c] + pair[c, k]
            copy = remote(
                partial.at[c, k - 1], across.at[c, k - 1],
                across_send.at[c, k - 1], across_recv.at[c, k - 1],
                {"yr": chip_at[k] * 2 + core},
            )
            copy.start()
            crossing.append(copy)

    def col(c, i):
        block = got.at[c, sta]
        return remote(
            block, block, col_send.at[c, i], col_recv.at[c, row],
            {"sta": rows_by[i] * minor + place},
        )

    def col_in(c, i):
        block = got.at[c, rows_by[i] * minor + place]
        return remote(
            block, block, col_send.at[c, i], col_recv.at[c, rows_by[i]],
            {"sta": rows_by[i] * minor + place},
        )

    def across_row(c, from_row, j):
        block = got.at[c, from_row * minor + place]
        return remote(
            block, block, row_send.at[c, from_row, j - 1], row_recv.at[c, from_row, j - 1],
            {"sta": row * minor + lax.rem(place + j, minor)},
        )

    def row_in(c, from_row, j):
        block = got.at[c, from_row * minor + lax.rem(place + minor - j, minor)]
        return remote(
            block, block, row_send.at[c, from_row, j - 1], row_recv.at[c, from_row, j - 1],
            {"sta": row * minor + lax.rem(place + minor - j, minor)},
        )

    def own(c):
        pairs[c * chips + chips - 1].wait_recv()
        total = sums_ref[yr, c] + pair[c, 0]
        for k in range(chips - 1):
            crossing[c * (chips - 1) + k].wait_recv()
            total = total + across[c, k]
        got[c, sta] = total
        for i in range(major - 1):
            col(c, i).start()
        for j in range(1, minor):
            across_row(c, row, j).start()

    def forward(c, then=lambda i: None):
        for i in range(major - 1):
            then(i)
            col_in(c, i).wait_recv()
            for j in range(1, minor):
                across_row(c, rows_by[i], j).start()
        then(major - 1)

    lane = iota((1, width), 1)
    mine = jnp.concatenate(
        [jnp.full((1, cell_pad), -1, I32)] + [cells_ref[h : h + 1] for h in range(halves)], axis=1
    )
    target = jnp.where(lane < cell_dev, lane + sta * cell_dev, mine)

    def build(first, last):
        for s in range(first, last):
            column = ids[s].T
            for h in range(halves):
                at = s * stations + h * LANES
                hot[at : at + LANES] = one_where(column[:, h : h + 1] == target)

    def cells(c):
        for j in range(1, minor):
            row_in(c, row, j).wait_recv()
            for i in range(major - 1):
                row_in(c, rows_by[i], j).wait_recv()
        for s in range(owners):
            sums = [got[c, s, k] for k in range(3)]
            high = [v.astype(BF16).astype(F32) for v in sums]
            low = [v - h for v, h in zip(sums, high)]
            tallies = [None] * 3
            for w, held in enumerate(words):
                word = got[c, s, 3 + w].astype(I32)
                for p, k in enumerate(held):
                    tallies[k] = ((word // base**p) & (base - 1)).astype(F32)
            parts = high + low + tallies
            if base > 256:
                rounded = [t.astype(BF16).astype(F32) for t in tallies]
                parts = high + low + rounded + [t - r for t, r in zip(tallies, rounded)]
            if len(parts) % 2:
                parts.append(jnp.zeros_like(parts[0]))
            lhs[:, s * stations : (s + 1) * stations] = jnp.concatenate(parts, axis=0).astype(BF16)
        total = dot(lhs[...], hot[...])
        step = 3 * TILE
        tally = total[2 * step : 3 * step]
        if base > 256:
            tally = tally + total[3 * step : 4 * step]
        clim = (total[:step] + total[step : 2 * step]) / jnp.maximum(tally, 1.0)
        out_ref[yr, c] = clim.reshape(3, TILE, width)
        block = out_ref.at[yr, c]
        for k in range(1, chips):
            far(c, k).start()
        near(c, 0).start()

    def far(c, k):
        block = out_ref.at[yr, c]
        return remote(
            block, block, far_send.at[c, k - 1], far_recv.at[c, k - 1],
            {"yr": chip_at[k] * 2 + core},
        )

    def near(c, k):
        block = out_ref.at[chip_from[k] * 2 + core, c]
        return remote(block, block, near_send.at[c, k], near_recv.at[c, k], partner)

    def hand_on(c):
        for k in range(1, chips):
            far(c, k).wait_recv()
            near(c, k).start()

    for c in range(chunks):
        own(c)
    for copy in id_copies:
        copy.wait_recv()
    share = -(-owners // major)
    forward(0, lambda i: build(i * share, min((i + 1) * share, owners)))
    for c in range(chunks):
        if c + 1 < chunks:
            forward(c + 1)
        cells(c)
        if c >= 2:
            hand_on(c - 2)
    for c in range(max(chunks - 2, 0), chunks):
        hand_on(c)
    for c in range(chunks):
        for k in range(chips):
            near(c, k).wait()
        for k in range(1, chips):
            far(c, k).wait_send()
        for i in range(major - 1):
            col(c, i).wait_send()
        for j in range(1, minor):
            across_row(c, row, j).wait_send()
            for i in range(major - 1):
                across_row(c, rows_by[i], j).wait_send()
    for copy in id_copies + pairs + crossing:
        copy.wait_send()


def anomaly_kernel(
    ranges, cell_dev, cell_pad, rows, masked_ref, code_ref, clim_ref,
    out_hbm, climatology_hbm, table, clim_buf, out_buf, clim_sem, out_sem,
):
    block_total, days = masked_ref.shape
    stations = clim_ref.shape[-1] - cell_pad
    for k in range(3):
        part = clim_ref[:, :, k, :, cell_pad:].reshape(days, stations)
        high, low = split_two(part)
        table[:days, k * stations : (k + 1) * stations] = high
        table[days:, k * stations : (k + 1) * stations] = low
    for j in range(cell_pad // LANES):
        for k in range(3):
            part = clim_ref[:, :, k, :, j * LANES : (j + 1) * LANES].reshape(days, LANES)
            last = min((j + 1) * LANES, cell_dev)
            clim_buf[j * LANES : last, k * days : (k + 1) * days] = part.T[: last - j * LANES]
    clim_copy = pltpu.make_async_copy(clim_buf, climatology_hbm, clim_sem.at[0])
    clim_copy.start()
    copies = []
    for i in range(block_total // rows):
        here = slice(i * rows, (i + 1) * rows)
        code = code_ref[here]
        segment = code >> 1
        lane = iota(code.shape, 1)
        hot = jnp.concatenate(
            [one_where(segment == lane + j * LANES) for j in range(3 * stations // LANES)], axis=1
        )
        found = dot(hot, table[...], ((1,), (1,)))
        clim = found[:, :days] + found[:, days:]
        out_buf[here] = masked_ref[here] - (code & 1).astype(F32) * clim
        copy = pltpu.make_async_copy(out_buf.at[here], out_hbm.at[here], out_sem.at[i])
        copy.start()
        copies.append(copy)
    for copy in [clim_copy] + copies:
        copy.wait()


def per_device(temps, day_bits, block_offset, block_counts, station_cell):
    owners, ranges = lax.axis_size("sta"), lax.axis_size("yr")
    stations = station_cell.shape[0]
    block_total, days = temps.shape
    cell_dev = CELLS // owners
    cell_pad = round_up(cell_dev, LANES)
    width = cell_pad + stations
    words, base = tally_words(ranges)
    groups = 3 + len(words)
    chunks = days // ranges // TILE
    rows = 1024 if block_total % 1024 == 0 else block_total
    major = 4 if owners % 4 == 0 else owners
    minor, chips = owners // major, ranges // 2
    dma = pltpu.SemaphoreType.DMA
    whole = pl.BlockSpec(memory_space=VMEM)
    hbm = pl.BlockSpec(memory_space=pltpu.HBM)

    inputs = [
        pltpu.with_memory_space_constraint(array, pltpu.HBM)
        for array in (
            temps, day_bits, block_offset.reshape(block_total // LANES, LANES), block_counts,
            station_cell.reshape(stations // LANES, LANES),
        )
    ]
    sums, masked, code, cells = pl.pallas_call(
        functools.partial(sums_kernel, ranges, rows),
        in_specs=[hbm] * 5,
        out_specs=[whole] * 4,
        out_shape=[
            jax.ShapeDtypeStruct((ranges, chunks, groups, TILE, stations), F32),
            jax.ShapeDtypeStruct((block_total, days), F32),
            jax.ShapeDtypeStruct((block_total, days), I32),
            jax.ShapeDtypeStruct((TILE, LANES), I32),
        ],
        scratch_shapes=[
            VMEM((day_bits.shape[0], block_total), I32),
            VMEM((block_total // LANES, LANES), I32),
            VMEM((1, stations), I32),
            VMEM((3 * stations, 2 * days), F32),
            VMEM((len(words) * stations, days), F32),
            dma((4,)), dma((block_total // rows,)),
        ],
        compiler_params=pltpu.CompilerParams(vmem_limit_bytes=40 * 1024 * 1024),
    )(*inputs)

    block = (groups, TILE, stations)
    parts = 3 * 3 if base <= 256 else 3 * 4
    crossings, others, sides = max(chips - 1, 1), max(major - 1, 1), max(minor - 1, 1)
    clim = pl.pallas_call(
        functools.partial(exchange_kernel, ranges, owners, major, cell_dev, cell_pad),
        in_specs=[whole] * 2,
        out_specs=whole,
        out_shape=jax.ShapeDtypeStruct((ranges, chunks, 3, TILE, width), F32),
        scratch_shapes=[
            VMEM((owners, TILE, LANES), I32),
            VMEM((chunks, chips) + block, F32),
            VMEM((chunks, crossings) + block, F32),
            VMEM((chunks, crossings) + block, F32),
            VMEM((chunks, owners) + block, F32),
            VMEM((round_up(parts * TILE, 16), owners * stations), BF16),
            VMEM((owners * stations, width), BF16),
            dma((owners - 1,)), dma((owners - 1,)),
            dma((chunks, chips)), dma((chunks, chips)),
            dma((chunks, crossings)), dma((chunks, crossings)),
            dma((chunks, others)), dma((chunks, major)),
            dma((chunks, major, sides)), dma((chunks, major, sides)),
            dma((chunks, crossings)), dma((chunks, crossings)),
            dma((chunks, chips)), dma((chunks, chips)),
        ],
        compiler_params=pltpu.CompilerParams(
            collective_id=0, has_side_effects=True, vmem_limit_bytes=40 * 1024 * 1024
        ),
    )(sums, cells)

    rows = 512 if block_total % 512 == 0 else block_total
    return pl.pallas_call(
        functools.partial(anomaly_kernel, ranges, cell_dev, cell_pad, rows),
        in_specs=[whole] * 3,
        out_specs=[hbm] * 2,
        out_shape=[
            jax.ShapeDtypeStruct((block_total, days), F32),
            jax.ShapeDtypeStruct((cell_dev, 3 * days), F32),
        ],
        scratch_shapes=[
            VMEM((2 * days, 3 * stations), BF16),
            VMEM((cell_dev, 3 * days), F32),
            VMEM((block_total, days), F32),
            dma((1,)), dma((block_total // rows,)),
        ],
        compiler_params=pltpu.CompilerParams(vmem_limit_bytes=40 * 1024 * 1024),
    )(masked, code, clim)


def solution(mesh):
    in_specs = (
        P(("sta", "yr"), None),
        P(None, ("sta", "yr")),
        P(("sta", "yr")),
        P("yr", "sta"),
        P("sta"),
    )
    out_specs = (P(("sta", "yr"), None), P("sta", None))

    def run(*args):
        return tuple(per_device(*args))

    return jax.shard_map(
        run, mesh=mesh, in_specs=in_specs, out_specs=out_specs, check_vma=False
    )
```

time: 67.3 us -> 51.2 us (0.76)
  Pallas kernels: 61.3 us -> 50.4 us
  local copies, waits for them, and re-layouts: 4.34 us -> 0 us
  other arithmetic: 0.68 us -> 0 us
    pallas_call x3 -> x2, Pallas kernels: 53.4 us -> 45.7 us  [the longest x1 37.6 us: per_device(): pl.pallas_call(functools.partial(exchange_kernel, ranges, owners, major,...]
    unnamed x10 -> x0, local copies, waits for them, and re-layouts: 4.2 us -> none
    pallas_call x1, Pallas kernels: 7.84 us -> 4.67 us  [per_device(): pl.pallas_call(functools.partial(anomaly_kernel, ranges, cell_dev, cell_p...]
    convert_element_type x1 -> x0, other arithmetic: 0.68 us -> none  [per_device(): station_cell.astype(F32).reshape(stations // LANES, LANES)]
where the time goes in v1:
time: 51.2 us; the launch traced here: 51.1 us
  Pallas kernels  50.4 us (98%)
  between operations  0.65 us (1%)
    pallas_call x1, Pallas kernels, per_device(): pl.pallas_call(functools.partial(exchange_kernel, ranges, owners, major,...  37.6 us
    pallas_call x1, Pallas kernels, per_device(): pl.pallas_call(functools.partial(sums_kernel, ranges, rows), in_specs=[hb...  8.15 us
    pallas_call x1, Pallas kernels, per_device(): pl.pallas_call(functools.partial(anomaly_kernel, ranges, cell_dev, cell_p...  4.67 us

profile of v1, /device:TPU:0, one launch (start us, length us, event | category | flops | bytes accessed | tf_op | source)
XLA Modules:
  0.0 51.1 jit_solution(1402299220059619926)
XLA Ops:
  0.6 8.2 %shard_map.68 = (f32[4,4,4,8,256]{4,3,2,1,0:T(8,128)S(1)}, f32[6144,128]{1,0:T(8,128)S(1)}, s32[6144,128]{1,0:T(8,128)S(1)}, s32[8,128]{1,0:T(8,128)S(1)}) custom-call(f32[6144,128]{1,0:T(8,128)} %temps_hbm.1, s32[4,6144]{1,0:T(4,128)} %bits_hbm.1, s32[48,128]{1,0:T(8,128)} %bitcast.2, s32[1,256]{1,0:T(1,128)} %counts_hbm.1, s32[2,128]{1,0:T(2,128)} %bitcast.3), custom_call_target="tpu_custom_call" | custom-call | tf_op jit(solution)/shard_map/pallas_call | solution.py:437
  8.8 37.6 %shard_map.69.clim_ref = f32[4,4,3,8,1664]{4,3,2,1,0:T(8,128)S(1)} custom-call(f32[4,4,4,8,256]{4,3,2,1,0:T(8,128)S(1)} %get-tuple-element.8.sums_ref, s32[8,128]{1,0:T(8,128)S(1)} %get-tuple-element.9.cells_ref), custom_call_target="tpu_custom_call" | custom-call | tf_op jit(solution)/shard_map/pallas_call | solution.py:461
  46.4 4.7 %shard_map.70 = (f32[6144,128]{1,0:T(8,128)}, f32[1296,384]{1,0:T(8,128)}) custom-call(f32[6144,128]{1,0:T(8,128)S(1)} %get-tuple-element.6.masked_ref, s32[6144,128]{1,0:T(8,128)S(1)} %get-tuple-element.7.code_ref, f32[4,4,3,8,1664]{4,3,2,1,0:T(8,128)S(1)} %shard_map.69.clim_ref), custom_call_target="tpu_custom_call" | custom-call | tf_op jit(solution)/shard_map/pallas_call | solution.py:488

commit v2 on v1

--- a/solution.py
+++ b/solution.py
@@ -12,6 +12,9 @@
 MOST_BLOCKS = 48
 LANES = 128
 TILE = 8
+GROUP = 16
+WINDOW = 256
+NEARBY = 96
 F32 = jnp.float32
 BF16 = jnp.bfloat16
 I32 = jnp.int32
@@ -89,68 +92,104 @@
     firsts[1].wait()
     offsets = offs[...]
     third = offsets - 3 * ((offsets * 21846) >> 16)
-    double_segment = 2 * (third * stations + station.astype(I32))
+    station = station.astype(I32)
+    segment = (station // GROUP) * (3 * GROUP) + third * GROUP + station % GROUP
+    double_segment = 2 * segment
     limit = CALENDAR - LANES * third
-    station_of = [jnp.where(third == k, station, -1.0).astype(BF16) for k in range(3)]
     weight_of = []
     for held in words:
         weight = jnp.zeros(third.shape, F32)
         for place, k in enumerate(held):
             weight = jnp.where(third == k, float(base**place), weight)
         weight_of.append(weight.astype(BF16))
-    station = station.astype(BF16)
-    at = iota((stations, LANES), 0).astype(F32).astype(BF16)
+    group = station // GROUP
+    per_step = rows // LANES
+    low = [jnp.min(group[i * per_step : (i + 1) * per_step]) for i in range(steps)]
+    high = [jnp.max(group[i * per_step : (i + 1) * per_step]) for i in range(steps)]
+    close = functools.reduce(jnp.logical_and, [h - l < WINDOW // (3 * GROUP) for l, h in zip(low, high)])
+    at = iota((WINDOW, LANES), 0).astype(F32).astype(BF16)
     day = iota((LANES, LANES), 0)
     shift = day & 31
     one, zero = jnp.ones((), BF16), jnp.zeros((), BF16)
+    acc[...] = jnp.zeros_like(acc)
+    tally[...] = jnp.zeros_like(tally)
     firsts[2].wait()
-    for i in range(steps):
-        loads[i].wait()
-        values, observed_all, hots, weights = [], [], [], []
-        for q in range(i * rows // LANES, (i + 1) * rows // LANES):
-            here = slice(q * LANES, (q + 1) * LANES)
-            packed = jnp.concatenate(
-                [jnp.broadcast_to(bits[w : w + 1, here], (32, LANES)) for w in range(bits.shape[0])],
-                axis=0,
-            )
-            bit = (packed >> shift) & 1
-            code = jnp.where(day < limit[q : q + 1], bit, 0) + double_segment[q : q + 1]
-            code = code.T
-            code_ref[here] = code
-            observed = (code & 1).astype(F32)
-            value = masked_ref[here] * observed
-            masked_ref[here] = value
-            values.append(jnp.concatenate(split_two(value), axis=1))
-            observed_all.append(observed.astype(BF16))
-            hots.append(
-                jnp.concatenate(
-                    [
-                        jnp.where(at == jnp.broadcast_to(s[q : q + 1], at.shape), one, zero)
-                        for s in station_of
-                    ],
-                    axis=0,
+    for q in range(blocks):
+        here = slice(q * LANES, (q + 1) * LANES)
+        packed = jnp.concatenate(
+            [jnp.broadcast_to(bits[w : w + 1, here], (32, LANES)) for w in range(bits.shape[0])],
+            axis=0,
+        )
+        bit = (packed >> shift) & 1
+        code = jnp.where(day < limit[q : q + 1], bit, 0) + double_segment[q : q + 1]
+        code_ref[here] = code.T
+    for copy in loads:
+        copy.wait()
+
+    def against(number, start, size):
+        return jnp.clip(number - start, -1, size).astype(F32).astype(BF16)
+
+    def spread(lines, q, size):
+        return jnp.broadcast_to(lines[q : q + 1], (size, LANES))
+
+    def add_up(windows_of, nearby_of):
+        for i in range(steps):
+            values, observed_all = [], []
+            blocks_here = range(i * per_step, (i + 1) * per_step)
+            for q in blocks_here:
+                here = slice(q * LANES, (q + 1) * LANES)
+                observed = (code_ref[here] & 1).astype(F32)
+                value = masked_ref[here] * observed
+                masked_ref[here] = value
+                values.append(jnp.concatenate(split_two(value), axis=1))
+                observed_all.append(observed.astype(BF16))
+            values = jnp.concatenate(values, axis=0)
+            observed_all = jnp.concatenate(observed_all, axis=0)
+            for start in windows_of(i):
+                place = against(segment, start, WINDOW)
+                hot = jnp.concatenate(
+                    [jnp.where(at == spread(place, q, WINDOW), one, zero) for q in blocks_here], axis=1
                 )
-            )
-            inside = at == jnp.broadcast_to(station[q : q + 1], at.shape)
-            weights.append(
-                jnp.concatenate(
-                    [
-                        jnp.where(inside, jnp.broadcast_to(w[q : q + 1], at.shape), zero)
-                        for w in weight_of
-                    ],
-                    axis=0,
-                )
-            )
-        total = dot(jnp.concatenate(hots, axis=1), jnp.concatenate(values, axis=0))
-        count = dot(jnp.concatenate(weights, axis=1), jnp.concatenate(observed_all, axis=0))
-        acc[...] = total if i == 0 else acc[...] + total
-        tally[...] = count if i == 0 else tally[...] + count
+                acc[pl.ds(start, WINDOW)] += dot(hot, values)
+            for start in nearby_of(i):
+                place = against(station, start, NEARBY)
+                for w, weight in enumerate(weight_of):
+                    hot = jnp.concatenate(
+                        [
+                            jnp.where(
+                                at[:NEARBY] == spread(place, q, NEARBY), spread(weight, q, NEARBY), zero
+                            )
+                            for q in blocks_here
+                        ],
+                        axis=1,
+                    )
+                    tally[w, pl.ds(start, NEARBY)] += dot(hot, observed_all)
+
+    @pl.when(close)
+    def _():
+        add_up(
+            lambda i: [pl.multiple_of(low[i] * (3 * GROUP), GROUP)],
+            lambda i: [pl.multiple_of(low[i] * GROUP, GROUP)],
+        )
+
+    @pl.when(jnp.logical_not(close))
+    def _():
+        add_up(
+            lambda i: range(0, 3 * stations, WINDOW), lambda i: range(0, stations, NEARBY)
+        )
+
     split = (ranges, chunk_count, TILE, stations)
     for k in range(3):
-        part = acc[k * stations : (k + 1) * stations]
+        part = jnp.concatenate(
+            [
+                acc[(3 * g + k) * GROUP : (3 * g + k + 1) * GROUP]
+                for g in range(stations // GROUP)
+            ],
+            axis=0,
+        )
         sums_ref[:, :, k] = (part[:, :LANES] + part[:, LANES:]).T.reshape(split)
     for w in range(len(words)):
-        sums_ref[:, :, 3 + w] = tally[w * stations : (w + 1) * stations].T.reshape(split)
+        sums_ref[:, :, 3 + w] = tally[w, :stations].T.reshape(split)
     firsts[3].wait()
 
 
@@ -176,15 +215,16 @@
 
 
 def exchange_kernel(
-    ranges, owners, major, cell_dev, cell_pad, sums_ref, cells_ref, out_ref,
-    ids, pair, partial, across, got, lhs, hot,
+    ranges, owners, major, cap, cell_dev, cell_pad, sums_ref, cells_ref, out_ref,
+    ids, pair, partial, across, got, lhs, hot, clim_ref, unpack,
     id_send, id_recv, pair_send, pair_recv, across_send, across_recv,
     col_send, col_recv, row_send, row_recv, far_send, far_recv, near_send, near_recv,
 ):
     _, chunks, groups, _, stations = sums_ref.shape
     halves = stations // LANES
     words, base = tally_words(ranges)
-    width = out_ref.shape[-1]
+    width = clim_ref.shape[-1]
+    slots = width - stations
     chips, minor = ranges // 2, owners // major
     sta, yr = lax.axis_index("sta"), lax.axis_index("yr")
     chip, core = yr // 2, lax.rem(yr, 2)
@@ -193,9 +233,15 @@
     chip_at = [lax.rem(chip + k, chips) for k in range(chips)]
     chip_from = [lax.rem(chip + chips - k, chips) for k in range(chips)]
     near_first = [
-        sorted((r for r in range(major) if r != mine), key=lambda r: (abs(r - mine), r))
+        sorted(
+            (r for r in range(major) if r != mine),
+            key=lambda r: (abs(r - mine), r if 2 * mine < major else -r),
+        )
         for mine in range(major)
     ]
+    relayed = major == 4
+    inner = (row == 1) | (row == 2)
+    turned = [relayed and c % 2 == 1 for c in range(chunks)]
     rows_by = [pick(row, [near_first[m][i] for m in range(major)]) for i in range(major - 1)]
 
     greet(
@@ -241,6 +287,20 @@
             {"sta": rows_by[i] * minor + place},
         )
 
+    def relay(c):
+        block = got.at[c, rows_by[-1] * minor + place]
+        return remote(
+            block, block, col_send.at[c, major - 1], col_recv.at[c, rows_by[-1]],
+            {"sta": rows_by[0] * minor + place},
+        )
+
+    def turn(c, j):
+        block = got.at[c, row * minor + lax.rem(place + minor - j, minor)]
+        return remote(
+            block, block, row_send.at[c, rows_by[0], j - 1], row_recv.at[c, row, j - 1],
+            {"sta": rows_by[0] * minor + place},
+        )
+
     def col_in(c, i):
         block = got.at[c, rows_by[i] * minor + place]
         return remote(
@@ -270,7 +330,10 @@
             total = total + across[c, k]
         got[c, sta] = total
         for i in range(major - 1):
-            col(c, i).start()
+            if relayed and i == major - 2:
+                pl.when(inner)(col(c, i).start)
+            else:
+                col(c, i).start()
         for j in range(1, minor):
             across_row(c, row, j).start()
 
@@ -278,18 +341,63 @@
         for i in range(major - 1):
             then(i)
             col_in(c, i).wait_recv()
+            if relayed and i == major - 2:
+                pl.when(inner)(relay(c).start)
             for j in range(1, minor):
-                across_row(c, rows_by[i], j).start()
+                if turned[c] and i == 0:
+                    row_in(c, row, j).wait_recv()
+                    turn(c, j).start()
+                else:
+                    across_row(c, rows_by[i], j).start()
         then(major - 1)
 
-    lane = iota((1, width), 1)
-    mine = jnp.concatenate(
-        [jnp.full((1, cell_pad), -1, I32)] + [cells_ref[h : h + 1] for h in range(halves)], axis=1
-    )
-    target = jnp.where(lane < cell_dev, lane + sta * cell_dev, mine)
-
-    def build(first, last):
-        for s in range(first, last):
+    first = sta * cell_dev
+    own_ids = [cells_ref[h : h + 1] for h in range(halves)]
+
+    def targets():
+        if not cap:
+            lane = iota((1, slots), 1)
+            return jnp.concatenate([jnp.where(lane < cell_dev, lane + first, -1)] + own_ids, axis=1)
+        local = jnp.concatenate([ids[s, :halves] for s in range(owners)], axis=0) - first
+        owned = (local >= 0) & (local < cell_dev)
+        flags = one_where(owned)
+        tile = (LANES, LANES)
+        rank = dot(flags, one_where(iota(tile, 0) < iota(tile, 1)))
+        held = dot(flags, jnp.ones(tile, BF16))
+        ranks = []
+        for s in range(owners):
+            for h in range(halves):
+                at = s * halves + h
+                ranks.append(sum([held[s * halves + g : s * halves + g + 1] for g in range(h)],
+                                 rank[at : at + 1]))
+        ranks = jnp.where(owned, jnp.concatenate(ranks, axis=0), -1.0).T
+        high, low = (local >> 8).astype(F32), (local & 255).astype(F32)
+        lane = iota((LANES, cap), 1).astype(F32)
+        found = []
+        for s in range(owners):
+            at = s * halves
+            place = jnp.concatenate(
+                [one_where(ranks[:, at + h : at + h + 1] == lane) for h in range(halves)], axis=0
+            )
+            line = [
+                jnp.concatenate([part[at + h : at + h + 1] for h in range(halves)], axis=1)
+                for part in (high, low)
+            ]
+            line.append(jnp.ones_like(line[0]))
+            line.append(jnp.zeros((TILE - 3, stations), F32))
+            got_line = dot(jnp.concatenate(line, axis=0).astype(BF16), place)
+            number = 256.0 * got_line[0:1] + got_line[1:2]
+            found.append(jnp.where(got_line[2:3] > 0.5, number, -1.0))
+        column = jnp.concatenate(found, axis=0).T
+        lane = iota((1, cell_pad), 1).astype(F32)
+        for s in range(owners):
+            unpack[s * cap : (s + 1) * cap] = one_where(column[:, s : s + 1] == lane)
+        known = jnp.concatenate(found, axis=1).astype(I32)
+        known = jnp.where(known >= 0, known + first, -1)
+        return jnp.concatenate([known] + own_ids, axis=1)
+
+    def build(target, low, high):
+        for s in range(low, high):
             column = ids[s].T
             for h in range(halves):
                 at = s * stations + h * LANES
@@ -297,7 +405,8 @@
 
     def cells(c):
         for j in range(1, minor):
-            row_in(c, row, j).wait_recv()
+            if not turned[c]:
+                row_in(c, row, j).wait_recv()
             for i in range(major - 1):
                 row_in(c, rows_by[i], j).wait_recv()
         for s in range(owners):
@@ -322,21 +431,20 @@
         if base > 256:
             tally = tally + total[3 * step : 4 * step]
         clim = (total[:step] + total[step : 2 * step]) / jnp.maximum(tally, 1.0)
-        out_ref[yr, c] = clim.reshape(3, TILE, width)
-        block = out_ref.at[yr, c]
+        clim_ref[yr, c] = clim.reshape(3, TILE, width)
         for k in range(1, chips):
             far(c, k).start()
         near(c, 0).start()
 
     def far(c, k):
-        block = out_ref.at[yr, c]
+        block = clim_ref.at[yr, c]
         return remote(
             block, block, far_send.at[c, k - 1], far_recv.at[c, k - 1],
             {"yr": chip_at[k] * 2 + core},
         )
 
     def near(c, k):
-        block = out_ref.at[chip_from[k] * 2 + core, c]
+        block = clim_ref.at[chip_from[k] * 2 + core, c]
         return remote(block, block, near_send.at[c, k], near_recv.at[c, k], partner)
 
     def hand_on(c):
@@ -344,27 +452,53 @@
             far(c, k).wait_recv()
             near(c, k).start()
 
-    for c in range(chunks):
-        own(c)
+    def expand(c):
+        for k in range(chips):
+            near(c, k).wait_recv()
+        both = clim_ref[:, c]
+        out_ref[:, c, :, :, cell_pad:] = both[..., slots:]
+        flat = both[..., :slots].reshape(ranges * 3 * TILE, slots)
+        if not cap:
+            out_ref[:, c, :, :, :cell_pad] = both[..., :slots]
+            return
+        rows = flat.shape[0]
+        ones = jnp.ones((2 * TILE, slots), BF16)
+        wide = dot(jnp.concatenate([*split_two(flat), ones], axis=0), unpack[...])
+        times = jnp.maximum(wide[2 * rows : 2 * rows + 1], 1.0)
+        cells_at = (wide[:rows] + wide[rows : 2 * rows]) / times
+        out_ref[:, c, :, :, :cell_pad] = cells_at.reshape(ranges, 3, TILE, cell_pad)
+
+    own(0)
     for copy in id_copies:
         copy.wait_recv()
+    target = targets()
+    for c in range(1, chunks):
+        own(c)
     share = -(-owners // major)
-    forward(0, lambda i: build(i * share, min((i + 1) * share, owners)))
+    forward(0, lambda i: build(target, i * share, min((i + 1) * share, owners)))
     for c in range(chunks):
         if c + 1 < chunks:
             forward(c + 1)
         cells(c)
         if c >= 2:
             hand_on(c - 2)
+        if c >= 3:
+            expand(c - 3)
     for c in range(max(chunks - 2, 0), chunks):
         hand_on(c)
+    for c in range(max(chunks - 3, 0), chunks):
+        expand(c)
     for c in range(chunks):
         for k in range(chips):
-            near(c, k).wait()
+            near(c, k).wait_send()
         for k in range(1, chips):
             far(c, k).wait_send()
         for i in range(major - 1):
-            col(c, i).wait_send()
+            if relayed and i == major - 2:
+                pl.when(inner)(col(c, i).wait_send)
+                pl.when(inner)(relay(c).wait_send)
+            else:
+                col(c, i).wait_send()
         for j in range(1, minor):
             across_row(c, row, j).wait_send()
             for i in range(major - 1):
@@ -379,33 +513,60 @@
 ):
     block_total, days = masked_ref.shape
     stations = clim_ref.shape[-1] - cell_pad
+    steps = block_total // rows
+    low, high = [], []
+    for i in range(steps):
+        ends = [code_ref[at : at + TILE] for at in (i * rows, (i + 1) * rows - TILE)]
+        low.append((jnp.min(ends[0]) >> 1) // (3 * GROUP))
+        high.append((jnp.max(ends[1]) >> 1) // (3 * GROUP))
+    close = functools.reduce(jnp.logical_and, [h - l < WINDOW // (3 * GROUP) for l, h in zip(low, high)])
     for k in range(3):
-        part = clim_ref[:, :, k, :, cell_pad:].reshape(days, stations)
-        high, low = split_two(part)
-        table[:days, k * stations : (k + 1) * stations] = high
-        table[days:, k * stations : (k + 1) * stations] = low
+        part = clim_ref[:, :, k, :, cell_pad:].reshape(days, stations).T
+        both = jnp.concatenate(split_two(part), axis=1)
+        for g in range(stations // GROUP):
+            at = (3 * g + k) * GROUP
+            table[at : at + GROUP] = both[g * GROUP : (g + 1) * GROUP]
+    table[3 * stations :] = jnp.zeros((table.shape[0] - 3 * stations, 2 * days), BF16)
+    clim_copy = pltpu.make_async_copy(clim_buf, climatology_hbm, clim_sem.at[0])
+    copies = [
+        pltpu.make_async_copy(
+            out_buf.at[i * rows : (i + 1) * rows], out_hbm.at[i * rows : (i + 1) * rows], out_sem.at[i]
+        )
+        for i in range(steps)
+    ]
     for j in range(cell_pad // LANES):
         for k in range(3):
             part = clim_ref[:, :, k, :, j * LANES : (j + 1) * LANES].reshape(days, LANES)
             last = min((j + 1) * LANES, cell_dev)
             clim_buf[j * LANES : last, k * days : (k + 1) * days] = part.T[: last - j * LANES]
-    clim_copy = pltpu.make_async_copy(clim_buf, climatology_hbm, clim_sem.at[0])
     clim_copy.start()
-    copies = []
-    for i in range(block_total // rows):
-        here = slice(i * rows, (i + 1) * rows)
-        code = code_ref[here]
-        segment = code >> 1
-        lane = iota(code.shape, 1)
-        hot = jnp.concatenate(
-            [one_where(segment == lane + j * LANES) for j in range(3 * stations // LANES)], axis=1
-        )
-        found = dot(hot, table[...], ((1,), (1,)))
-        clim = found[:, :days] + found[:, days:]
-        out_buf[here] = masked_ref[here] - (code & 1).astype(F32) * clim
-        copy = pltpu.make_async_copy(out_buf.at[here], out_hbm.at[here], out_sem.at[i])
-        copy.start()
-        copies.append(copy)
+
+    def subtract(windows_of):
+        lane = iota((rows, LANES), 1)
+        for i in range(steps):
+            here = slice(i * rows, (i + 1) * rows)
+            code = code_ref[here]
+            segment = code >> 1
+            found = None
+            for start in windows_of(i):
+                place = segment - start
+                hot = jnp.concatenate(
+                    [one_where(place == lane + j) for j in range(0, WINDOW, LANES)], axis=1
+                )
+                part = dot(hot, table[pl.ds(start, WINDOW)])
+                found = part if found is None else found + part
+            clim = found[:, :days] + found[:, days:]
+            out_buf[here] = masked_ref[here] - (code & 1).astype(F32) * clim
+            copies[i].start()
+
+    @pl.when(close)
+    def _():
+        subtract(lambda i: [pl.multiple_of(low[i] * (3 * GROUP), GROUP)])
+
+    @pl.when(jnp.logical_not(close))
+    def _():
+        subtract(lambda i: range(0, 3 * stations, WINDOW))
+
     for copy in [clim_copy] + copies:
         copy.wait()
 
@@ -421,6 +582,10 @@
     groups = 3 + len(words)
     chunks = days // ranges // TILE
     rows = 1024 if block_total % 1024 == 0 else block_total
+    cap = 4 * stations // owners
+    if cap % LANES or owners * cap >= cell_pad:
+        cap = 0
+    slots = owners * cap if cap else cell_pad
     major = 4 if owners % 4 == 0 else owners
     minor, chips = owners // major, ranges // 2
     dma = pltpu.SemaphoreType.DMA
@@ -448,8 +613,8 @@
             VMEM((day_bits.shape[0], block_total), I32),
             VMEM((block_total // LANES, LANES), I32),
             VMEM((1, stations), I32),
-            VMEM((3 * stations, 2 * days), F32),
-            VMEM((len(words) * stations, days), F32),
+            VMEM((round_up(3 * stations, WINDOW) + WINDOW, 2 * days), F32),
+            VMEM((len(words), stations + 2 * NEARBY, days), F32),
             dma((4,)), dma((block_total // rows,)),
         ],
         compiler_params=pltpu.CompilerParams(vmem_limit_bytes=40 * 1024 * 1024),
@@ -457,9 +622,9 @@
 
     block = (groups, TILE, stations)
     parts = 3 * 3 if base <= 256 else 3 * 4
-    crossings, others, sides = max(chips - 1, 1), max(major - 1, 1), max(minor - 1, 1)
+    crossings, sides = max(chips - 1, 1), max(minor - 1, 1)
     clim = pl.pallas_call(
-        functools.partial(exchange_kernel, ranges, owners, major, cell_dev, cell_pad),
+        functools.partial(exchange_kernel, ranges, owners, major, cap, cell_dev, cell_pad),
         in_specs=[whole] * 2,
         out_specs=whole,
         out_shape=jax.ShapeDtypeStruct((ranges, chunks, 3, TILE, width), F32),
@@ -470,11 +635,13 @@
             VMEM((chunks, crossings) + block, F32),
             VMEM((chunks, owners) + block, F32),
             VMEM((round_up(parts * TILE, 16), owners * stations), BF16),
-            VMEM((owners * stations, width), BF16),
+            VMEM((owners * stations, slots + stations), BF16),
+            VMEM((ranges, chunks, 3, TILE, slots + stations), F32),
+            VMEM((slots, cell_pad) if cap else (2 * TILE, LANES), BF16),
             dma((owners - 1,)), dma((owners - 1,)),
             dma((chunks, chips)), dma((chunks, chips)),
             dma((chunks, crossings)), dma((chunks, crossings)),
-            dma((chunks, others)), dma((chunks, major)),
+            dma((chunks, major)), dma((chunks, major)),
             dma((chunks, major, sides)), dma((chunks, major, sides)),
             dma((chunks, crossings)), dma((chunks, crossings)),
             dma((chunks, chips)), dma((chunks, chips)),
@@ -494,7 +661,7 @@
             jax.ShapeDtypeStruct((cell_dev, 3 * days), F32),
         ],
         scratch_shapes=[
-            VMEM((2 * days, 3 * stations), BF16),
+            VMEM((round_up(3 * stations, WINDOW) + WINDOW, 2 * days), BF16),
             VMEM((cell_dev, 3 * days), F32),
             VMEM((block_total, days), F32),
             dma((1,)), dma((block_total // rows,)),

time: 51.2 us -> 45.5 us (0.89)
  Pallas kernels: 50.4 us -> 44.5 us
    pallas_call x1, Pallas kernels: 8.15 us -> 4.94 us  [per_device(): pl.pallas_call(functools.partial(sums_kernel, ranges, rows), in_specs=[hb...]
    pallas_call x1, Pallas kernels: 4.67 us -> 3.24 us  [per_device(): pl.pallas_call(functools.partial(anomaly_kernel, ranges, cell_dev, cell_p...]
    pallas_call x1, Pallas kernels: 37.6 us -> 36.4 us  [per_device(): pl.pallas_call(functools.partial(exchange_kernel, ranges, owners, major,...]
where the time goes in v2:
time: 45.5 us; the launch traced here: 45.4 us
  Pallas kernels  44.5 us (98%)
  between operations  0.83 us (2%)
    pallas_call x1, Pallas kernels, per_device(): pl.pallas_call(functools.partial(exchange_kernel, ranges, owners, major,...  36.4 us
    pallas_call x1, Pallas kernels, per_device(): pl.pallas_call(functools.partial(sums_kernel, ranges, rows), in_specs=[hb...  4.94 us
    pallas_call x1, Pallas kernels, per_device(): pl.pallas_call(functools.partial(anomaly_kernel, ranges, cell_dev, cell_p...  3.24 us

profile of v2, /device:TPU:0, one launch (start us, length us, event | category | flops | bytes accessed | tf_op | source)
XLA Modules:
  0.0 45.4 jit_solution(6527383137865526827)
XLA Ops:
  0.6 4.9 %shard_map.68 = (f32[4,4,4,8,256]{4,3,2,1,0:T(8,128)S(1)}, f32[6144,128]{1,0:T(8,128)S(1)}, s32[6144,128]{1,0:T(8,128)S(1)}, s32[8,128]{1,0:T(8,128)S(1)}) custom-call(f32[6144,128]{1,0:T(8,128)} %temps_hbm.1, s32[4,6144]{1,0:T(4,128)} %bits_hbm.1, s32[48,128]{1,0:T(8,128)} %bitcast.2, s32[1,256]{1,0:T(1,128)} %counts_hbm.1, s32[2,128]{1,0:T(2,128)} %bitcast.3), custom_call_target="tpu_custom_call" | custom-call | tf_op jit(solution)/shard_map/pallas_call | solution.py:602
  5.6 36.4 %shard_map.69.clim_ref = f32[4,4,3,8,1664]{4,3,2,1,0:T(8,128)S(1)} custom-call(f32[4,4,4,8,256]{4,3,2,1,0:T(8,128)S(1)} %get-tuple-element.8.sums_ref, s32[8,128]{1,0:T(8,128)S(1)} %get-tuple-element.9.cells_ref), custom_call_target="tpu_custom_call" | custom-call | tf_op jit(solution)/shard_map/pallas_call | solution.py:626
  41.9 3.2 %shard_map.70 = (f32[6144,128]{1,0:T(8,128)}, f32[1296,384]{1,0:T(8,128)}) custom-call(f32[6144,128]{1,0:T(8,128)S(1)} %get-tuple-element.6.masked_ref, s32[6144,128]{1,0:T(8,128)S(1)} %get-tuple-element.7.code_ref, f32[4,4,3,8,1664]{4,3,2,1,0:T(8,128)S(1)} %shard_map.69.clim_ref), custom_call_target="tpu_custom_call" | custom-call | tf_op jit(solution)/shard_map/pallas_call | solution.py:655

commit v3 on v2

--- a/solution.py
+++ b/solution.py
@@ -200,11 +200,8 @@
     )
 
 
-def greet(peers):
-    barrier = pltpu.get_barrier_semaphore()
-    for where in peers:
-        pl.semaphore_signal(barrier, inc=1, device_id=where, device_id_type=pl.DeviceIdType.MESH)
-    pl.semaphore_wait(barrier, len(peers))
+def signal(semaphore, where):
+    pl.semaphore_signal(semaphore, inc=1, device_id=where, device_id_type=pl.DeviceIdType.MESH)
 
 
 def pick(index, table):
@@ -215,14 +212,15 @@
 
 
 def exchange_kernel(
-    ranges, owners, major, cap, cell_dev, cell_pad, sums_ref, cells_ref, out_ref,
-    ids, pair, partial, across, got, lhs, hot, clim_ref, unpack,
-    id_send, id_recv, pair_send, pair_recv, across_send, across_recv,
+    ranges, owners, major, cell_dev, cell_pad, sums_ref, cells_ref, clim_ref,
+    ids, pair, partial, across, got, lhs, started, hot,
+    ready, further, pair_send, pair_recv, across_send, across_recv,
     col_send, col_recv, row_send, row_recv, far_send, far_recv, near_send, near_recv,
 ):
     _, chunks, groups, _, stations = sums_ref.shape
     halves = stations // LANES
     words, base = tally_words(ranges)
+    base_bits = base.bit_length() - 1
     width = clim_ref.shape[-1]
     slots = width - stations
     chips, minor = ranges // 2, owners // major
@@ -241,22 +239,76 @@
     ]
     relayed = major == 4
     inner = (row == 1) | (row == 2)
-    turned = [relayed and c % 2 == 1 for c in range(chunks)]
+    relays = [relayed and 0 < c < chunks for c in range(chunks + 1)]
+    turned = [relayed and c % 2 == 1 for c in range(chunks)] + [False]
     rows_by = [pick(row, [near_first[m][i] for m in range(major)]) for i in range(major - 1)]
 
-    greet(
-        [partner]
-        + [{"yr": c * 2 + core} for c in chip_at[1:]]
-        + [{"sta": lax.rem(sta + j, owners)} for j in range(1, owners)]
-    )
-    id_copies = []
-    for j in range(1, owners):
-        copy = remote(
-            cells_ref, ids.at[sta], id_send.at[j - 1], id_recv.at[j - 1],
-            {"sta": lax.rem(sta + j, owners)},
-        )
-        copy.start()
-        id_copies.append(copy)
+    barrier = pltpu.get_barrier_semaphore()
+    beside = [{"sta": row * minor + lax.rem(place + j, minor)} for j in range(1, minor)]
+    near_peers = [partner] + [{"yr": c * 2 + core} for c in chip_at[1:]] + beside
+    steps_by = [(row > 0, row - 1), (row < major - 1, row + 1)] if relayed else []
+    if not relayed:
+        near_peers += [{"sta": r * minor + place} for r in rows_by]
+    for where in near_peers:
+        signal(barrier, where)
+    neighbours = pick(row, [1] + [2] * (major - 2) + [1]) if relayed else 0
+    for able, to_row in steps_by:
+        pl.when(able)(functools.partial(signal, barrier, {"sta": to_row * minor + place}))
+    pl.semaphore_wait(barrier, len(near_peers) + neighbours)
+    for able, to_row in steps_by:
+        pl.when(able)(functools.partial(signal, ready, {"sta": to_row * minor + place}))
+    def view(c, owner):
+        return got.at[c, owner] if c < chunks else ids.at[owner]
+
+    def send_own(c, which):
+        for i in which:
+            if relays[c] and i == major - 2:
+                pl.when(inner)(col(c, i).start)
+            else:
+                col(c, i).start()
+
+    def col(c, i):
+        block = view(c, sta)
+        return remote(
+            block, block, col_send.at[c, i], col_recv.at[c, row],
+            {"sta": rows_by[i] * minor + place},
+        )
+
+    def relay(c):
+        block = view(c, rows_by[-1] * minor + place)
+        return remote(
+            block, block, col_send.at[c, major - 1], col_recv.at[c, rows_by[-1]],
+            {"sta": rows_by[0] * minor + place},
+        )
+
+    def turn(c, j):
+        block = view(c, row * minor + lax.rem(place + minor - j, minor))
+        return remote(
+            block, block, row_send.at[c, rows_by[0], j - 1], row_recv.at[c, row, j - 1],
+            {"sta": rows_by[0] * minor + place},
+        )
+
+    def col_in(c, i):
+        block = view(c, rows_by[i] * minor + place)
+        return remote(
+            block, block, col_send.at[c, i], col_recv.at[c, rows_by[i]],
+            {"sta": rows_by[i] * minor + place},
+        )
+
+    def across_row(c, from_row, j):
+        block = view(c, from_row * minor + place)
+        return remote(
+            block, block, row_send.at[c, from_row, j - 1], row_recv.at[c, from_row, j - 1],
+            {"sta": row * minor + lax.rem(place + j, minor)},
+        )
+
+    def row_in(c, from_row, j):
+        block = view(c, from_row * minor + lax.rem(place + minor - j, minor))
+        return remote(
+            block, block, row_send.at[c, from_row, j - 1], row_recv.at[c, from_row, j - 1],
+            {"sta": row * minor + lax.rem(place + minor - j, minor)},
+        )
+
     pairs = []
     for c in range(chunks):
         for k in [*range(1, chips), 0]:
@@ -267,6 +319,9 @@
             copy.start()
             pairs.append(copy)
     ids[sta] = cells_ref[...]
+    send_own(chunks, [0])
+    for j in range(1, minor):
+        across_row(chunks, row, j).start()
     crossing = []
     for c in range(chunks):
         for k in range(1, chips):
@@ -280,48 +335,6 @@
             copy.start()
             crossing.append(copy)
 
-    def col(c, i):
-        block = got.at[c, sta]
-        return remote(
-            block, block, col_send.at[c, i], col_recv.at[c, row],
-            {"sta": rows_by[i] * minor + place},
-        )
-
-    def relay(c):
-        block = got.at[c, rows_by[-1] * minor + place]
-        return remote(
-            block, block, col_send.at[c, major - 1], col_recv.at[c, rows_by[-1]],
-            {"sta": rows_by[0] * minor + place},
-        )
-
-    def turn(c, j):
-        block = got.at[c, row * minor + lax.rem(place + minor - j, minor)]
-        return remote(
-            block, block, row_send.at[c, rows_by[0], j - 1], row_recv.at[c, row, j - 1],
-            {"sta": rows_by[0] * minor + place},
-        )
-
-    def col_in(c, i):
-        block = got.at[c, rows_by[i] * minor + place]
-        return remote(
-            block, block, col_send.at[c, i], col_recv.at[c, rows_by[i]],
-            {"sta": rows_by[i] * minor + place},
-        )
-
-    def across_row(c, from_row, j):
-        block = got.at[c, from_row * minor + place]
-        return remote(
-            block, block, row_send.at[c, from_row, j - 1], row_recv.at[c, from_row, j - 1],
-            {"sta": row * minor + lax.rem(place + j, minor)},
-        )
-
-    def row_in(c, from_row, j):
-        block = got.at[c, from_row * minor + lax.rem(place + minor - j, minor)]
-        return remote(
-            block, block, row_send.at[c, from_row, j - 1], row_recv.at[c, from_row, j - 1],
-            {"sta": row * minor + lax.rem(place + minor - j, minor)},
-        )
-
     def own(c):
         pairs[c * chips + chips - 1].wait_recv()
         total = sums_ref[yr, c] + pair[c, 0]
@@ -329,103 +342,76 @@
             crossing[c * (chips - 1) + k].wait_recv()
             total = total + across[c, k]
         got[c, sta] = total
-        for i in range(major - 1):
-            if relayed and i == major - 2:
-                pl.when(inner)(col(c, i).start)
-            else:
-                col(c, i).start()
+        send_own(c, range(major - 1))
         for j in range(1, minor):
             across_row(c, row, j).start()
 
-    def forward(c, then=lambda i: None):
+    def pass_on(c, i):
+        col_in(c, i).wait_recv()
+        if relays[c] and i == major - 2:
+            pl.when(inner)(relay(c).start)
+        for j in range(1, minor):
+            if turned[c] and i == 0:
+                row_in(c, row, j).wait_recv()
+                turn(c, j).start()
+            else:
+                across_row(c, rows_by[i], j).start()
+
+    def forward(c):
         for i in range(major - 1):
-            then(i)
-            col_in(c, i).wait_recv()
-            if relayed and i == major - 2:
-                pl.when(inner)(relay(c).start)
-            for j in range(1, minor):
-                if turned[c] and i == 0:
-                    row_in(c, row, j).wait_recv()
-                    turn(c, j).start()
-                else:
-                    across_row(c, rows_by[i], j).start()
-        then(major - 1)
-
-    first = sta * cell_dev
-    own_ids = [cells_ref[h : h + 1] for h in range(halves)]
-
-    def targets():
-        if not cap:
-            lane = iota((1, slots), 1)
-            return jnp.concatenate([jnp.where(lane < cell_dev, lane + first, -1)] + own_ids, axis=1)
-        local = jnp.concatenate([ids[s, :halves] for s in range(owners)], axis=0) - first
-        owned = (local >= 0) & (local < cell_dev)
-        flags = one_where(owned)
-        tile = (LANES, LANES)
-        rank = dot(flags, one_where(iota(tile, 0) < iota(tile, 1)))
-        held = dot(flags, jnp.ones(tile, BF16))
-        ranks = []
-        for s in range(owners):
-            for h in range(halves):
-                at = s * halves + h
-                ranks.append(sum([held[s * halves + g : s * halves + g + 1] for g in range(h)],
-                                 rank[at : at + 1]))
-        ranks = jnp.where(owned, jnp.concatenate(ranks, axis=0), -1.0).T
-        high, low = (local >> 8).astype(F32), (local & 255).astype(F32)
-        lane = iota((LANES, cap), 1).astype(F32)
-        found = []
-        for s in range(owners):
-            at = s * halves
-            place = jnp.concatenate(
-                [one_where(ranks[:, at + h : at + h + 1] == lane) for h in range(halves)], axis=0
-            )
-            line = [
-                jnp.concatenate([part[at + h : at + h + 1] for h in range(halves)], axis=1)
-                for part in (high, low)
-            ]
-            line.append(jnp.ones_like(line[0]))
-            line.append(jnp.zeros((TILE - 3, stations), F32))
-            got_line = dot(jnp.concatenate(line, axis=0).astype(BF16), place)
-            number = 256.0 * got_line[0:1] + got_line[1:2]
-            found.append(jnp.where(got_line[2:3] > 0.5, number, -1.0))
-        column = jnp.concatenate(found, axis=0).T
-        lane = iota((1, cell_pad), 1).astype(F32)
-        for s in range(owners):
-            unpack[s * cap : (s + 1) * cap] = one_where(column[:, s : s + 1] == lane)
-        known = jnp.concatenate(found, axis=1).astype(I32)
-        known = jnp.where(known >= 0, known + first, -1)
-        return jnp.concatenate([known] + own_ids, axis=1)
-
-    def build(target, low, high):
-        for s in range(low, high):
-            column = ids[s].T
-            for h in range(halves):
-                at = s * stations + h * LANES
-                hot[at : at + LANES] = one_where(column[:, h : h + 1] == target)
-
-    def cells(c):
+            pass_on(c, i)
+
+    def side_in(c):
         for j in range(1, minor):
             if not turned[c]:
                 row_in(c, row, j).wait_recv()
             for i in range(major - 1):
                 row_in(c, rows_by[i], j).wait_recv()
-        for s in range(owners):
-            sums = [got[c, s, k] for k in range(3)]
-            high = [v.astype(BF16).astype(F32) for v in sums]
-            low = [v - h for v, h in zip(sums, high)]
+
+    owner_at = [
+        r * minor + lax.rem(place + j, minor) for j in range(minor) for r in [row] + rows_by
+    ]
+
+    first = sta * cell_dev
+    own_ids = [cells_ref[h : h + 1] for h in range(halves)]
+
+    lane = iota((1, slots), 1)
+    target = jnp.concatenate([jnp.where(lane < cell_dev, lane + first, -1)] + own_ids, axis=1)
+
+    def build(low, high):
+        for s in range(low, high):
+            column = ids[owner_at[s]].T
+            for h in range(halves):
+                at = s * stations + h * LANES
+                hot[at : at + LANES] = one_where(column[:, h : h + 1] == target)
+
+    def add_shards(c, low, high):
+        for s in range(low, high):
+            owner = owner_at[s]
+            sums = [got[c, owner, k] for k in range(3)]
+            high_part = [v.astype(BF16).astype(F32) for v in sums]
+            low_part = [v - h for v, h in zip(sums, high_part)]
             tallies = [None] * 3
             for w, held in enumerate(words):
-                word = got[c, s, 3 + w].astype(I32)
+                word = got[c, owner, 3 + w].astype(I32)
                 for p, k in enumerate(held):
-                    tallies[k] = ((word // base**p) & (base - 1)).astype(F32)
-            parts = high + low + tallies
+                    tallies[k] = ((word >> (p * base_bits)) & (base - 1)).astype(F32)
+            parts = high_part + low_part + tallies
             if base > 256:
                 rounded = [t.astype(BF16).astype(F32) for t in tallies]
-                parts = high + low + rounded + [t - r for t, r in zip(tallies, rounded)]
+                parts = high_part + low_part + rounded + [t - r for t, r in zip(tallies, rounded)]
             if len(parts) % 2:
                 parts.append(jnp.zeros_like(parts[0]))
             lhs[:, s * stations : (s + 1) * stations] = jnp.concatenate(parts, axis=0).astype(BF16)
-        total = dot(lhs[...], hot[...])
+        here = slice(low * stations, high * stations)
+        return dot(lhs[:, here], hot[here])
+
+    def cells_start(c):
+        started[...] = add_shards(c, 0, major)
+
+    def cells(c):
+        side_in(c)
+        total = started[...] + add_shards(c, major, owners) if minor > 1 else started[...]
         step = 3 * TILE
         tally = total[2 * step : 3 * step]
         if base > 256:
@@ -452,49 +438,54 @@
             far(c, k).wait_recv()
             near(c, k).start()
 
-    def expand(c):
-        for k in range(chips):
-            near(c, k).wait_recv()
-        both = clim_ref[:, c]
-        out_ref[:, c, :, :, cell_pad:] = both[..., slots:]
-        flat = both[..., :slots].reshape(ranges * 3 * TILE, slots)
-        if not cap:
-            out_ref[:, c, :, :, :cell_pad] = both[..., :slots]
-            return
-        rows = flat.shape[0]
-        ones = jnp.ones((2 * TILE, slots), BF16)
-        wide = dot(jnp.concatenate([*split_two(flat), ones], axis=0), unpack[...])
-        times = jnp.maximum(wide[2 * rows : 2 * rows + 1], 1.0)
-        cells_at = (wide[:rows] + wide[rows : 2 * rows]) / times
-        out_ref[:, c, :, :, :cell_pad] = cells_at.reshape(ranges, 3, TILE, cell_pad)
-
-    own(0)
-    for copy in id_copies:
-        copy.wait_recv()
-    target = targets()
-    for c in range(1, chunks):
+    if relayed:
+        pl.semaphore_wait(ready, neighbours)
+        for able, to_row in steps_by:
+            pl.when(able)(functools.partial(signal, further, {"sta": to_row * minor + place}))
+        pl.semaphore_wait(further, neighbours)
+    send_own(chunks, range(1, major - 1))
+    last = major - 2
+    for c in range(min(chunks, 2)):
         own(c)
-    share = -(-owners // major)
-    forward(0, lambda i: build(target, i * share, min((i + 1) * share, owners)))
+        if c < last:
+            pass_on(chunks, c)
+    for i in range(min(chunks, 2, last), last + 1):
+        pass_on(chunks, i)
+    for i in range(last):
+        pass_on(0, i)
+    if chunks > 2:
+        own(2)
+    build(0, last + 1)
+    pass_on(0, last)
+    for c in range(3, chunks):
+        own(c)
+    build(last + 1, major)
+    cells_start(0)
+    if chunks > 1:
+        for i in range(major - 2):
+            pass_on(1, i)
+    side_in(chunks)
+    build(major, owners)
+    if chunks > 1:
+        pass_on(1, major - 2)
     for c in range(chunks):
-        if c + 1 < chunks:
+        if c > 0 and c + 1 < chunks:
             forward(c + 1)
         cells(c)
+        if c + 1 < chunks:
+            cells_start(c + 1)
         if c >= 2:
             hand_on(c - 2)
-        if c >= 3:
-            expand(c - 3)
     for c in range(max(chunks - 2, 0), chunks):
         hand_on(c)
-    for c in range(max(chunks - 3, 0), chunks):
-        expand(c)
     for c in range(chunks):
         for k in range(chips):
-            near(c, k).wait_send()
+            near(c, k).wait()
         for k in range(1, chips):
             far(c, k).wait_send()
+    for c in range(chunks + 1):
         for i in range(major - 1):
-            if relayed and i == major - 2:
+            if relays[c] and i == major - 2:
                 pl.when(inner)(col(c, i).wait_send)
                 pl.when(inner)(relay(c).wait_send)
             else:
@@ -503,7 +494,7 @@
             across_row(c, row, j).wait_send()
             for i in range(major - 1):
                 across_row(c, rows_by[i], j).wait_send()
-    for copy in id_copies + pairs + crossing:
+    for copy in pairs + crossing:
         copy.wait_send()
 
 
@@ -582,10 +573,6 @@
     groups = 3 + len(words)
     chunks = days // ranges // TILE
     rows = 1024 if block_total % 1024 == 0 else block_total
-    cap = 4 * stations // owners
-    if cap % LANES or owners * cap >= cell_pad:
-        cap = 0
-    slots = owners * cap if cap else cell_pad
     major = 4 if owners % 4 == 0 else owners
     minor, chips = owners // major, ranges // 2
     dma = pltpu.SemaphoreType.DMA
@@ -624,7 +611,7 @@
     parts = 3 * 3 if base <= 256 else 3 * 4
     crossings, sides = max(chips - 1, 1), max(minor - 1, 1)
     clim = pl.pallas_call(
-        functools.partial(exchange_kernel, ranges, owners, major, cap, cell_dev, cell_pad),
+        functools.partial(exchange_kernel, ranges, owners, major, cell_dev, cell_pad),
         in_specs=[whole] * 2,
         out_specs=whole,
         out_shape=jax.ShapeDtypeStruct((ranges, chunks, 3, TILE, width), F32),
@@ -635,14 +622,13 @@
             VMEM((chunks, crossings) + block, F32),
             VMEM((chunks, owners) + block, F32),
             VMEM((round_up(parts * TILE, 16), owners * stations), BF16),
-            VMEM((owners * stations, slots + stations), BF16),
-            VMEM((ranges, chunks, 3, TILE, slots + stations), F32),
-            VMEM((slots, cell_pad) if cap else (2 * TILE, LANES), BF16),
-            dma((owners - 1,)), dma((owners - 1,)),
+            VMEM((round_up(parts * TILE, 16), width), F32),
+            VMEM((owners * stations, width), BF16),
+            pltpu.SemaphoreType.REGULAR, pltpu.SemaphoreType.REGULAR,
             dma((chunks, chips)), dma((chunks, chips)),
             dma((chunks, crossings)), dma((chunks, crossings)),
-            dma((chunks, major)), dma((chunks, major)),
-            dma((chunks, major, sides)), dma((chunks, major, sides)),
+            dma((chunks + 1, major)), dma((chunks + 1, major)),
+            dma((chunks + 1, major, sides)), dma((chunks + 1, major, sides)),
             dma((chunks, crossings)), dma((chunks, crossings)),
             dma((chunks, chips)), dma((chunks, chips)),
         ],

time: 45.5 us -> 44.7 us (0.982)
  Pallas kernels: 44.5 us -> 43.6 us
    pallas_call x1, Pallas kernels: 36.4 us -> 35.6 us  [per_device(): pl.pallas_call(functools.partial(exchange_kernel, ranges, owners, major,...]
where the time goes in v3:
time: 44.7 us; the launch traced here: 44.4 us
  Pallas kernels  43.6 us (98%)
  between operations  0.81 us (2%)
    pallas_call x1, Pallas kernels, per_device(): pl.pallas_call(functools.partial(exchange_kernel, ranges, owners, major,...  35.6 us
    pallas_call x1, Pallas kernels, per_device(): pl.pallas_call(functools.partial(sums_kernel, ranges, rows), in_specs=[hb...  4.76 us
    pallas_call x1, Pallas kernels, per_device(): pl.pallas_call(functools.partial(anomaly_kernel, ranges, cell_dev, cell_p...  3.24 us

profile of v3, /device:TPU:0, one launch (start us, length us, event | category | flops | bytes accessed | tf_op | source)
XLA Modules:
  0.0 44.4 jit_solution(1552513860004122629)
XLA Ops:
  0.6 4.8 %shard_map.68 = (f32[4,4,4,8,256]{4,3,2,1,0:T(8,128)S(1)}, f32[6144,128]{1,0:T(8,128)S(1)}, s32[6144,128]{1,0:T(8,128)S(1)}, s32[8,128]{1,0:T(8,128)S(1)}) custom-call(f32[6144,128]{1,0:T(8,128)} %temps_hbm.1, s32[4,6144]{1,0:T(4,128)} %bits_hbm.1, s32[48,128]{1,0:T(8,128)} %bitcast.2, s32[1,256]{1,0:T(1,128)} %counts_hbm.1, s32[2,128]{1,0:T(2,128)} %bitcast.3), custom_call_target="tpu_custom_call" | custom-call | tf_op jit(solution)/shard_map/pallas_call | solution.py:589
  5.4 35.6 %shard_map.69.clim_ref = f32[4,4,3,8,1664]{4,3,2,1,0:T(8,128)S(1)} custom-call(f32[4,4,4,8,256]{4,3,2,1,0:T(8,128)S(1)} %get-tuple-element.8.sums_ref, s32[8,128]{1,0:T(8,128)S(1)} %get-tuple-element.9.cells_ref), custom_call_target="tpu_custom_call" | custom-call | tf_op jit(solution)/shard_map/pallas_call | solution.py:613
  41.0 3.2 %shard_map.70 = (f32[6144,128]{1,0:T(8,128)}, f32[1296,384]{1,0:T(8,128)}) custom-call(f32[6144,128]{1,0:T(8,128)S(1)} %get-tuple-element.6.masked_ref, s32[6144,128]{1,0:T(8,128)S(1)} %get-tuple-element.7.code_ref, f32[4,4,3,8,1664]{4,3,2,1,0:T(8,128)S(1)} %shard_map.69.clim_ref), custom_call_target="tpu_custom_call" | custom-call | tf_op jit(solution)/shard_map/pallas_call | solution.py:641

commit v4 on v3

--- a/solution.py
+++ b/solution.py
@@ -204,6 +204,12 @@
     pl.semaphore_signal(semaphore, inc=1, device_id=where, device_id_type=pl.DeviceIdType.MESH)
 
 
+def chunk_plan(chips, chunks):
+    if chips == 2 and chunks > 1:
+        return chunks - 1, chunks + 1
+    return chunks, chunks
+
+
 def pick(index, table):
     value = jnp.int32(table[0])
     for i in range(1, len(table)):
@@ -224,6 +230,8 @@
     width = clim_ref.shape[-1]
     slots = width - stations
     chips, minor = ranges // 2, owners // major
+    shared, total_chunks = chunk_plan(chips, chunks)
+    id_index = total_chunks
     sta, yr = lax.axis_index("sta"), lax.axis_index("yr")
     chip, core = yr // 2, lax.rem(yr, 2)
     row, place = sta // minor, lax.rem(sta, minor)
@@ -239,8 +247,8 @@
     ]
     relayed = major == 4
     inner = (row == 1) | (row == 2)
-    relays = [relayed and 0 < c < chunks for c in range(chunks + 1)]
-    turned = [relayed and c % 2 == 1 for c in range(chunks)] + [False]
+    relays = [relayed and 0 < c < id_index for c in range(id_index + 1)]
+    turned = [relayed and c > 0 and c != 2 for c in range(id_index)] + [False]
     rows_by = [pick(row, [near_first[m][i] for m in range(major)]) for i in range(major - 1)]
 
     barrier = pltpu.get_barrier_semaphore()
@@ -258,7 +266,7 @@
     for able, to_row in steps_by:
         pl.when(able)(functools.partial(signal, ready, {"sta": to_row * minor + place}))
     def view(c, owner):
-        return got.at[c, owner] if c < chunks else ids.at[owner]
+        return got.at[c, owner] if c < id_index else ids.at[owner]
 
     def send_own(c, which):
         for i in which:
@@ -319,9 +327,9 @@
             copy.start()
             pairs.append(copy)
     ids[sta] = cells_ref[...]
-    send_own(chunks, [0])
+    send_own(id_index, [0])
     for j in range(1, minor):
-        across_row(chunks, row, j).start()
+        across_row(id_index, row, j).start()
     crossing = []
     for c in range(chunks):
         for k in range(1, chips):
@@ -335,14 +343,30 @@
             copy.start()
             crossing.append(copy)
 
+    if total_chunks > chunks:
+        c = chunks - 1
+        pairs[c * chips + chips - 1].wait_recv()
+        partial[chunks, 0] = sums_ref[yr, c] + pair[c, 0]
+        copy = remote(
+            partial.at[chunks, 0], across.at[chunks, 0],
+            across_send.at[chunks, 0], across_recv.at[chunks, 0], {"yr": chip_at[1] * 2 + core},
+        )
+        copy.start()
+        crossing.append(copy)
+
     def own(c):
-        pairs[c * chips + chips - 1].wait_recv()
-        total = sums_ref[yr, c] + pair[c, 0]
+        if c == chunks:
+            total = partial[c - 1, 0]
+        elif c == chunks - 1 and total_chunks > chunks:
+            total = partial[chunks, 0]
+        else:
+            pairs[c * chips + chips - 1].wait_recv()
+            total = sums_ref[yr, c] + pair[c, 0]
         for k in range(chips - 1):
             crossing[c * (chips - 1) + k].wait_recv()
             total = total + across[c, k]
         got[c, sta] = total
-        send_own(c, range(major - 1))
+        send_own(c, range(major - 2, -1, -1))
         for j in range(1, minor):
             across_row(c, row, j).start()
 
@@ -417,9 +441,15 @@
         if base > 256:
             tally = tally + total[3 * step : 4 * step]
         clim = (total[:step] + total[step : 2 * step]) / jnp.maximum(tally, 1.0)
-        clim_ref[yr, c] = clim.reshape(3, TILE, width)
-        for k in range(1, chips):
-            far(c, k).start()
+        clim = clim.reshape(3, TILE, width)
+        if c == chunks:
+            clim_ref[chip_at[1] * 2 + core, c - 1] = clim
+            near(c - 1, 1).start()
+            return
+        clim_ref[yr, c] = clim
+        if c < shared:
+            for k in range(1, chips):
+                far(c, k).start()
         near(c, 0).start()
 
     def far(c, k):
@@ -443,47 +473,51 @@
         for able, to_row in steps_by:
             pl.when(able)(functools.partial(signal, further, {"sta": to_row * minor + place}))
         pl.semaphore_wait(further, neighbours)
-    send_own(chunks, range(1, major - 1))
+    send_own(id_index, range(1, major - 1))
     last = major - 2
     for c in range(min(chunks, 2)):
         own(c)
         if c < last:
-            pass_on(chunks, c)
+            pass_on(id_index, c)
     for i in range(min(chunks, 2, last), last + 1):
-        pass_on(chunks, i)
+        pass_on(id_index, i)
     for i in range(last):
         pass_on(0, i)
     if chunks > 2:
         own(2)
     build(0, last + 1)
     pass_on(0, last)
-    for c in range(3, chunks):
+    for c in range(3, total_chunks):
         own(c)
     build(last + 1, major)
     cells_start(0)
     if chunks > 1:
         for i in range(major - 2):
             pass_on(1, i)
-    side_in(chunks)
+    side_in(id_index)
     build(major, owners)
     if chunks > 1:
         pass_on(1, major - 2)
-    for c in range(chunks):
-        if c > 0 and c + 1 < chunks:
+    handed = 0
+    for c in range(total_chunks):
+        if c > 0 and c + 1 < total_chunks:
             forward(c + 1)
+        if c >= 3 and handed < shared:
+            hand_on(handed)
+            handed += 1
         cells(c)
-        if c + 1 < chunks:
+        if c + 1 < total_chunks:
             cells_start(c + 1)
-        if c >= 2:
-            hand_on(c - 2)
-    for c in range(max(chunks - 2, 0), chunks):
+    for c in range(handed, shared):
         hand_on(c)
     for c in range(chunks):
         for k in range(chips):
             near(c, k).wait()
+        if c >= shared:
+            continue
         for k in range(1, chips):
             far(c, k).wait_send()
-    for c in range(chunks + 1):
+    for c in range(id_index + 1):
         for i in range(major - 1):
             if relays[c] and i == major - 2:
                 pl.when(inner)(col(c, i).wait_send)
@@ -609,6 +643,7 @@
 
     block = (groups, TILE, stations)
     parts = 3 * 3 if base <= 256 else 3 * 4
+    total_chunks = chunk_plan(chips, chunks)[1]
     crossings, sides = max(chips - 1, 1), max(minor - 1, 1)
     clim = pl.pallas_call(
         functools.partial(exchange_kernel, ranges, owners, major, cell_dev, cell_pad),
@@ -618,17 +653,17 @@
         scratch_shapes=[
             VMEM((owners, TILE, LANES), I32),
             VMEM((chunks, chips) + block, F32),
-            VMEM((chunks, crossings) + block, F32),
-            VMEM((chunks, crossings) + block, F32),
-            VMEM((chunks, owners) + block, F32),
+            VMEM((total_chunks, crossings) + block, F32),
+            VMEM((total_chunks, crossings) + block, F32),
+            VMEM((total_chunks, owners) + block, F32),
             VMEM((round_up(parts * TILE, 16), owners * stations), BF16),
             VMEM((round_up(parts * TILE, 16), width), F32),
             VMEM((owners * stations, width), BF16),
             pltpu.SemaphoreType.REGULAR, pltpu.SemaphoreType.REGULAR,
             dma((chunks, chips)), dma((chunks, chips)),
-            dma((chunks, crossings)), dma((chunks, crossings)),
-            dma((chunks + 1, major)), dma((chunks + 1, major)),
-            dma((chunks + 1, major, sides)), dma((chunks + 1, major, sides)),
+            dma((total_chunks, crossings)), dma((total_chunks, crossings)),
+            dma((total_chunks + 1, major)), dma((total_chunks + 1, major)),
+            dma((total_chunks + 1, major, sides)), dma((total_chunks + 1, major, sides)),
             dma((chunks, crossings)), dma((chunks, crossings)),
             dma((chunks, chips)), dma((chunks, chips)),
         ],

time: 44.7 us -> 44 us (0.984)
  Pallas kernels: 43.6 us -> 43 us
    pallas_call x1, Pallas kernels: 35.6 us -> 35 us  [per_device(): pl.pallas_call(functools.partial(exchange_kernel, ranges, owners, major,...]
where the time goes in v4:
time: 44 us; the launch traced here: 43.8 us
  Pallas kernels  43 us (98%)
  between operations  0.81 us (2%)
    pallas_call x1, Pallas kernels, per_device(): pl.pallas_call(functools.partial(exchange_kernel, ranges, owners, major,...  35 us
    pallas_call x1, Pallas kernels, per_device(): pl.pallas_call(functools.partial(sums_kernel, ranges, rows), in_specs=[hb...  4.76 us
    pallas_call x1, Pallas kernels, per_device(): pl.pallas_call(functools.partial(anomaly_kernel, ranges, cell_dev, cell_p...  3.24 us

profile of v4, /device:TPU:0, one launch (start us, length us, event | category | flops | bytes accessed | tf_op | source)
XLA Modules:
  0.0 43.8 jit_solution(6182523581272978725)
XLA Ops:
  0.6 4.8 %shard_map.68 = (f32[4,4,4,8,256]{4,3,2,1,0:T(8,128)S(1)}, f32[6144,128]{1,0:T(8,128)S(1)}, s32[6144,128]{1,0:T(8,128)S(1)}, s32[8,128]{1,0:T(8,128)S(1)}) custom-call(f32[6144,128]{1,0:T(8,128)} %temps_hbm.1, s32[4,6144]{1,0:T(4,128)} %bits_hbm.1, s32[48,128]{1,0:T(8,128)} %bitcast.2, s32[1,256]{1,0:T(1,128)} %counts_hbm.1, s32[2,128]{1,0:T(2,128)} %bitcast.3), custom_call_target="tpu_custom_call" | custom-call | tf_op jit(solution)/shard_map/pallas_call | solution.py:623
  5.4 35.0 %shard_map.69.clim_ref = f32[4,4,3,8,1664]{4,3,2,1,0:T(8,128)S(1)} custom-call(f32[4,4,4,8,256]{4,3,2,1,0:T(8,128)S(1)} %get-tuple-element.8.sums_ref, s32[8,128]{1,0:T(8,128)S(1)} %get-tuple-element.9.cells_ref), custom_call_target="tpu_custom_call" | custom-call | tf_op jit(solution)/shard_map/pallas_call | solution.py:648
  40.4 3.2 %shard_map.70 = (f32[6144,128]{1,0:T(8,128)}, f32[1296,384]{1,0:T(8,128)}) custom-call(f32[6144,128]{1,0:T(8,128)S(1)} %get-tuple-element.6.masked_ref, s32[6144,128]{1,0:T(8,128)S(1)} %get-tuple-element.7.code_ref, f32[4,4,3,8,1664]{4,3,2,1,0:T(8,128)S(1)} %shard_map.69.clim_ref), custom_call_target="tpu_custom_call" | custom-call | tf_op jit(solution)/shard_map/pallas_call | solution.py:676

commit v5 on v4

--- a/solution.py
+++ b/solution.py
@@ -487,7 +487,7 @@
         own(2)
     build(0, last + 1)
     pass_on(0, last)
-    for c in range(3, total_chunks):
+    for c in range(3, chunks):
         own(c)
     build(last + 1, major)
     cells_start(0)
@@ -508,6 +508,8 @@
         cells(c)
         if c + 1 < total_chunks:
             cells_start(c + 1)
+        if c == 0 and total_chunks > chunks:
+            own(chunks)
     for c in range(handed, shared):
         hand_on(c)
     for c in range(chunks):

time: 44 us -> 44.7 us (1.016)
  Pallas kernels: 43 us -> 43.7 us
    pallas_call x1, Pallas kernels: 35 us -> 35.7 us  [per_device(): pl.pallas_call(functools.partial(exchange_kernel, ranges, owners, major,...]
where the time goes in v5:
time: 44.7 us; the launch traced here: 44.5 us
  Pallas kernels  43.7 us (98%)
  between operations  0.81 us (2%)
    pallas_call x1, Pallas kernels, per_device(): pl.pallas_call(functools.partial(exchange_kernel, ranges, owners, major,...  35.7 us
    pallas_call x1, Pallas kernels, per_device(): pl.pallas_call(functools.partial(sums_kernel, ranges, rows), in_specs=[hb...  4.76 us
    pallas_call x1, Pallas kernels, per_device(): pl.pallas_call(functools.partial(anomaly_kernel, ranges, cell_dev, cell_p...  3.24 us

profile of v5, /device:TPU:0, one launch (start us, length us, event | category | flops | bytes accessed | tf_op | source)
XLA Modules:
  0.0 44.5 jit_solution(4997769114542299686)
XLA Ops:
  0.6 4.8 %shard_map.68 = (f32[4,4,4,8,256]{4,3,2,1,0:T(8,128)S(1)}, f32[6144,128]{1,0:T(8,128)S(1)}, s32[6144,128]{1,0:T(8,128)S(1)}, s32[8,128]{1,0:T(8,128)S(1)}) custom-call(f32[6144,128]{1,0:T(8,128)} %temps_hbm.1, s32[4,6144]{1,0:T(4,128)} %bits_hbm.1, s32[48,128]{1,0:T(8,128)} %bitcast.2, s32[1,256]{1,0:T(1,128)} %counts_hbm.1, s32[2,128]{1,0:T(2,128)} %bitcast.3), custom_call_target="tpu_custom_call" | custom-call | tf_op jit(solution)/shard_map/pallas_call | solution.py:625
  5.4 35.7 %shard_map.69.clim_ref = f32[4,4,3,8,1664]{4,3,2,1,0:T(8,128)S(1)} custom-call(f32[4,4,4,8,256]{4,3,2,1,0:T(8,128)S(1)} %get-tuple-element.8.sums_ref, s32[8,128]{1,0:T(8,128)S(1)} %get-tuple-element.9.cells_ref), custom_call_target="tpu_custom_call" | custom-call | tf_op jit(solution)/shard_map/pallas_call | solution.py:650
  41.1 3.2 %shard_map.70 = (f32[6144,128]{1,0:T(8,128)}, f32[1296,384]{1,0:T(8,128)}) custom-call(f32[6144,128]{1,0:T(8,128)S(1)} %get-tuple-element.6.masked_ref, s32[6144,128]{1,0:T(8,128)S(1)} %get-tuple-element.7.code_ref, f32[4,4,3,8,1664]{4,3,2,1,0:T(8,128)S(1)} %shard_map.69.clim_ref), custom_call_target="tpu_custom_call" | custom-call | tf_op jit(solution)/shard_map/pallas_call | solution.py:678
